TPU v7x, 32 devices: a whole 2x2x4 slice. The times are simulated.
32 devices in a mesh: ta: 4 (over y, core), gx: 2 (over x), gy: 4 (over z).
Axes of the slice: x: 2, y: 2, z: 4, core: 2. Of those that a mesh axis runs over, the one named last changes fastest.
Arguments:
- space_links: float32 [3, 2, 3, 3, 4, 4, 2304], P(None, None, None, None, 'ta', 'gx', 'gy'), may hold values from -1 to 1, as said below
- time_links: float32 [2, 3, 3, 4, 4, 2304], P(None, None, None, 'ta', 'gx', 'gy'), may hold values from -1 to 1, as said below
- start_gauge: float32 [2, 3, 3, 4, 4, 2304], P(None, None, None, 'ta', 'gx', 'gy'), may hold values from -1 to 1, as said below
Outputs:
- gauge_field: float32 [2, 3, 3, 4, 4, 2304], P(None, None, None, 'ta', 'gx', 'gy')
- time_rotated: float32 [2, 3, 3, 4, 4, 2304], P(None, None, None, 'ta', 'gx', 'gy')
- functional: float32 [4, 4], P(None, 'ta')
- theta: float32 [4], P('ta')
Inputs may be any that keep to these rules, and one draw needn't show every extreme that they name: `space_links`: at every site the matrix is special unitary. `time_links`: at every site the matrix is special unitary. `start_gauge`: at every site the matrix is special unitary.
All inputs are finite; a program needn't handle non-finite values.
Results may differ from a plain program's by a relative error of at most 0.00021.
Values sent between devices are 32-bit elements; how exact they have to be, the bound alone decides.
No kernel may reach another device: no remote copies, remote signals or barrier semaphores. Data moves between devices by JAX's collectives and lax.ppermute only.
A program may use at most 64 MiB of HBM per device.

v0:
```python
import math

import jax
import jax.numpy as jnp
from jax import lax
from jax.experimental import pallas as pl
from jax.experimental.pallas import tpu as pltpu
from jax.sharding import PartitionSpec as P

NZ = 48
ITERS = 4

OMEGA = 1.7
FLOOR = 0.5
PAIRS = ((0, 1), (1, 2), (0, 2))

LANES = 128
HALF = LANES // 2
BLOCK_ROWS = LANES // math.gcd(NZ, LANES)
TILES = BLOCK_ROWS * NZ // LANES
BLOCK = BLOCK_ROWS * NZ
WINDOW = 4
LINK_PARTS = 36
PARTS = 48
GAUGE_AT = LINK_PARTS
ROW_Y = 12


def part_index(part):
    matrix, rest = divmod(part, 12)
    reim, rest = divmod(rest, 6)
    return matrix, reim * 9 + rest


def pack_kernel(own_tiles, links, gauge, own, below, above):
    width = gauge.shape[-1]
    lane = lax.broadcasted_iota(jnp.int32, (2, width), 1)
    odd = (lane // NZ + lane % NZ) % 2 == 1
    low = lax.broadcasted_iota(jnp.int32, (2, LANES), 1) < HALF
    extra_below = 0
    extra_above = 0
    for part in range(PARTS):
        matrix, entry = part_index(part)
        both = links[matrix * 18 + entry] if matrix < 3 else gauge[entry]
        swapped = jnp.concatenate([both[1:2], both[0:1]], axis=0)
        packed = jnp.where(odd, swapped, both)
        last = width - (own_tiles - 1) * LANES
        tiles = [packed[:, t * LANES : (t + 1) * LANES] for t in range(own_tiles - 1)]
        tiles.append(
            jnp.concatenate(
                [packed[:, width - last :], jnp.zeros((2, LANES - last), jnp.float32)], axis=1
            )
        )
        turned = [pltpu.roll(tile, HALF, 1) for tile in tiles]
        for t in range(own_tiles):
            shifted = jnp.where(low, turned[t - 1] if t else turned[0], turned[t])
            own[pl.ds((part * own_tiles + t) * 2, 2), :] = shifted
        first = own_tiles - 1 - TILES
        edge = jnp.where(low, tiles[own_tiles - 1], tiles[first])
        for t in range(TILES):
            body = edge if t == 0 else tiles[first + t]
            below[pl.ds((part * TILES + t) * 2, 2), :] = body
            above[pl.ds((part * TILES + t) * 2, 2), :] = tiles[t]
        if ROW_Y <= part < ROW_Y + 12 or part >= GAUGE_AT:
            below[pl.ds(PARTS * TILES * 2 + extra_below, 1), :] = tiles[first][1:2]
            extra_below += 1
        if part >= GAUGE_AT:
            above[pl.ds(PARTS * TILES * 2 + extra_above, 1), :] = tiles[TILES][1:2]
            extra_above += 1
    rest = above.shape[0] - (PARTS * TILES * 2 + extra_above)
    above[pl.ds(above.shape[0] - rest, rest), :] = jnp.zeros((rest, LANES), jnp.float32)


def pack(links, gauge):
    width = gauge.shape[-1]
    own_tiles = -(-width // LANES)
    rows = PARTS * TILES * 2
    shapes = [
        jax.ShapeDtypeStruct((PARTS * own_tiles * 2, LANES), jnp.float32),
        jax.ShapeDtypeStruct((rows + 24, LANES), jnp.float32),
        jax.ShapeDtypeStruct((rows + 16, LANES), jnp.float32),
    ]
    return pl.pallas_call(
        lambda *refs: pack_kernel(own_tiles, *refs),
        out_shape=shapes,
        name="pack",
    )(links, gauge)


def row_roll(value, shift):
    return pltpu.roll(value, shift % value.shape[0], 0)


def lane_roll(value, shift):
    return pltpu.roll(value, shift % LANES, 1)


class Masks:
    def __init__(self, rows):
        self.rows = rows
        self.lane = lax.broadcasted_iota(jnp.int32, (rows, LANES), 1)
        self.block = lax.broadcasted_iota(jnp.int32, (rows, LANES), 0) % WINDOW

    def z(self, tile):
        return (self.lane + tile * LANES) % NZ

    def odd(self, tile):
        return ((self.lane + tile * LANES) // NZ + self.z(tile)) % 2 == 1

    def owned(self, tile, start, width):
        place = self.block * BLOCK + tile * LANES + self.lane
        return (place >= start) & (place < start + width)


def y_ahead(tiles, masks):
    turned = [lane_roll(tile, -NZ) for tile in tiles]
    turned.append(row_roll(turned[0], -1))
    inside = masks.lane < LANES - NZ
    return [jnp.where(inside, turned[j], turned[j + 1]) for j in range(TILES)]


def y_behind(tiles, masks):
    turned = [lane_roll(tile, NZ) for tile in tiles]
    before = row_roll(turned[TILES - 1], 1)
    inside = masks.lane >= NZ
    return [jnp.where(inside, turned[j], turned[j - 1] if j else before) for j in range(TILES)]


def z_ahead(tiles, masks):
    step = [lane_roll(tile, -1) for tile in tiles]
    wrap = [lane_roll(tile, NZ - 1) for tile in tiles]
    out = []
    for j in range(TILES):
        near = step[j]
        if j < TILES - 1:
            near = jnp.where(masks.lane < LANES - 1, step[j], step[j + 1])
        far = wrap[j]
        if j:
            far = jnp.where(masks.lane >= NZ - 1, wrap[j], wrap[j - 1])
        out.append(jnp.where(masks.z(j) == NZ - 1, far, near))
    return out


def z_behind(tiles, masks):
    step = [lane_roll(tile, 1) for tile in tiles]
    wrap = [lane_roll(tile, 1 - NZ) for tile in tiles]
    out = []
    for j in range(TILES):
        near = step[j]
        if j:
            near = jnp.where(masks.lane >= 1, step[j], step[j - 1])
        far = wrap[j]
        if j < TILES - 1:
            far = jnp.where(masks.lane < LANES - NZ + 1, wrap[j], wrap[j + 1])
        out.append(jnp.where(masks.z(j) == 0, far, near))
    return out


def tile_of(j):
    return slice(j * LANES, (j + 1) * LANES)


def times_dagger(total, left, right):
    left_re, left_im = left
    right_re, right_im = right
    out_re = []
    out_im = []
    for a in range(3):
        for b in range(3):
            re = None if total is None else total[0][3 * a + b]
            im = None if total is None else total[1][3 * a + b]
            for c in range(3):
                lr, li = left_re[3 * a + c], left_im[3 * a + c]
                rr, ri = right_re[3 * b + c], right_im[3 * b + c]
                term = lr * rr
                re = term if re is None else re + term
                re = re + li * ri
                term = li * rr
                im = term if im is None else im + term
                im = im - lr * ri
            out_re.append(re)
            out_im.append(im)
    return out_re, out_im


def times(left, right):
    left_re, left_im = left
    right_re, right_im = right
    out_re = []
    out_im = []
    for a in range(3):
        for b in range(3):
            re = im = None
            for c in range(3):
                lr, li = left_re[3 * a + c], left_im[3 * a + c]
                rr, ri = right_re[3 * c + b], right_im[3 * c + b]
                re = lr * rr if re is None else re + lr * rr
                re = re - li * ri
                im = lr * ri if im is None else im + lr * ri
                im = im + li * rr
            out_re.append(re)
            out_im.append(im)
    return out_re, out_im


def relax_coeffs(moment, one, two):
    re, im = moment
    c0 = re[4 * one] + re[4 * two]
    c1 = -(im[3 * one + two] + im[3 * two + one])
    c2 = re[3 * two + one] - re[3 * one + two]
    c3 = im[4 * two] - im[4 * one]
    length = jnp.sqrt(c0 * c0 + c1 * c1 + c2 * c2 + c3 * c3)
    v0 = (1.0 - OMEGA) * length + OMEGA * c0
    v1 = OMEGA * c1
    v2 = OMEGA * c2
    v3 = OMEGA * c3
    scale = lax.rsqrt(jnp.maximum(v0 * v0 + v1 * v1 + v2 * v2 + v3 * v3, FLOOR * FLOOR))
    return v0 * scale, v1 * scale, v2 * scale, v3 * scale


def turn_rows(matrix, one, two, coeffs):
    a0, a1, a2, a3 = coeffs
    re = list(matrix[0])
    im = list(matrix[1])
    for col in range(3):
        f, s = 3 * one + col, 3 * two + col
        fr, fi, sr, si = re[f], im[f], re[s], im[s]
        re[f] = (a0 * fr - a3 * fi) + (a2 * sr - a1 * si)
        im[f] = (a0 * fi + a3 * fr) + (a2 * si + a1 * sr)
        re[s] = (a0 * sr + a3 * si) - (a2 * fr + a1 * fi)
        im[s] = (a0 * si - a3 * sr) + (a1 * fr - a2 * fi)
    return re, im


def antihermitian_squares(moment):
    re, im = moment
    total = None
    for a, b in PAIRS:
        dr = re[3 * a + b] - re[3 * b + a]
        di = im[3 * a + b] + im[3 * b + a]
        term = dr * dr + di * di
        total = term if total is None else total + term
    third = (im[0] + im[4] + im[8]) * (1.0 / 3.0)
    total = 0.5 * total
    for a in range(3):
        part = im[4 * a] - third
        total = total + part * part
    return total


def sweep_kernel(pairs, own_tiles, width, *refs):
    own = refs[0:pairs]
    below = refs[pairs : 2 * pairs]
    above = refs[2 * pairs : 3 * pairs]
    gauge_out, sums_out = refs[3 * pairs : 3 * pairs + 2]
    flat, extra, link, staple_link, field, moved, scores = refs[3 * pairs + 2 :]
    rows = pairs * WINDOW
    per_pair = WINDOW * TILES
    stride = pairs * per_pair
    start = WINDOW * BLOCK - width - (WINDOW * BLOCK - 2 * width)
    first_own = start // LANES
    masks = Masks(rows)

    for part in range(PARTS):
        for colour in range(2):
            for p in range(pairs):
                base = (colour * PARTS + part) * stride + p * per_pair
                flat[pl.ds(base + 1, TILES), :] = below[p][
                    pl.ds(part * TILES * 2 + colour, TILES, stride=2), :
                ]
                flat[pl.ds(base + first_own, own_tiles), :] = own[p][
                    pl.ds(part * own_tiles * 2 + colour, own_tiles, stride=2), :
                ]
                flat[pl.ds(base + per_pair - TILES, TILES), :] = above[p][
                    pl.ds(part * TILES * 2 + colour, TILES, stride=2), :
                ]
    for p in range(pairs):
        for i in range(24):
            extra[pl.ds(i * rows + WINDOW * p, 1), :] = below[p][pl.ds(PARTS * TILES * 2 + i, 1), :]
        for i in range(12):
            ahead = WINDOW * ((p + 1) % pairs)
            extra[pl.ds((24 + i) * rows + ahead, 1), :] = above[p][
                pl.ds(PARTS * TILES * 2 + i, 1), :
            ]

    first_block = masks.block == 0
    low_lanes = masks.lane < HALF
    low_second = (masks.block == 1) & low_lanes
    low_first = first_block & low_lanes

    def loaded(colour, part, j):
        base = (colour * PARTS + part) * stride
        value = flat[pl.ds(base + j, rows, stride=TILES), :]
        edge_y = ROW_Y <= part < ROW_Y + 12
        edge_g = part >= GAUGE_AT
        if j == 0:
            fill = jnp.zeros_like(value)
            if colour == 1 and edge_g:
                fill = extra[pl.ds((24 + part - GAUGE_AT) * rows, rows), :]
            value = jnp.where(first_block, fill, value)
        if j == 1:
            value = jnp.where(low_second, row_roll(value, 1), value)
            if colour == 1 and (edge_y or edge_g):
                at = part - ROW_Y if edge_y else 12 + part - GAUGE_AT
                value = jnp.where(low_first, extra[pl.ds(at * rows, rows), :], value)
        return value

    for colour in range(2):
        for matrix in range(4):
            target = link if matrix < 3 else field
            at = (colour * 3 + matrix) * 18 if matrix < 3 else colour * 18
            for j in range(TILES):
                parts = [loaded(colour, matrix * 12 + i, j) for i in range(12)]
                ar, br = parts[0:3], parts[3:6]
                ai, bi = parts[6:9], parts[9:12]
                for i in range(3):
                    target[at + i, :, tile_of(j)] = ar[i]
                    target[at + 3 + i, :, tile_of(j)] = br[i]
                    target[at + 9 + i, :, tile_of(j)] = ai[i]
                    target[at + 12 + i, :, tile_of(j)] = bi[i]
                    k, n = (i + 1) % 3, (i + 2) % 3
                    third_re = (ar[k] * br[n] - ai[k] * bi[n]) - (ar[n] * br[k] - ai[n] * bi[k])
                    third_im = (ar[n] * bi[k] + ai[n] * br[k]) - (ar[k] * bi[n] + ai[k] * br[n])
                    target[at + 6 + i, :, tile_of(j)] = third_re
                    target[at + 15 + i, :, tile_of(j)] = third_im

    def read(ref, at):
        return [ref[at, :, tile_of(j)] for j in range(TILES)]

    def write(ref, at, tiles):
        for j in range(TILES):
            ref[at, :, tile_of(j)] = tiles[j]

    for colour in range(2):
        for reim in range(2):
            for a in range(3):
                for c in range(3):
                    here = reim * 9 + 3 * a + c
                    there = reim * 9 + 3 * c + a
                    sign = -1.0 if reim else 1.0
                    ours = read(link, (colour * 3) * 18 + here)
                    theirs = [sign * t for t in read(link, ((1 - colour) * 3) * 18 + there)]
                    behind = [row_roll(t, WINDOW) for t in theirs]
                    same = []
                    other = []
                    for j in range(TILES):
                        lower = masks.odd(j) if colour else ~masks.odd(j)
                        same.append(jnp.where(lower, ours[j], theirs[j]))
                        other.append(jnp.where(lower, behind[j], ours[j]))
                    write(staple_link, (colour * 4 + 0) * 18 + here, same)
                    write(staple_link, (colour * 4 + 1) * 18 + here, other)
                    theirs = [sign * t for t in read(link, ((1 - colour) * 3 + 1) * 18 + there)]
                    write(staple_link, (colour * 4 + 2) * 18 + here, y_behind(theirs, masks))
                    theirs = [sign * t for t in read(link, ((1 - colour) * 3 + 2) * 18 + there)]
                    write(staple_link, (colour * 4 + 3) * 18 + here, z_behind(theirs, masks))

    def move(colour):
        for i in range(18):
            tiles = read(field, colour * 18 + i)
            behind = [row_roll(t, WINDOW) for t in tiles]
            if 2 * WINDOW == rows:
                other = behind
            else:
                other = []
                for j in range(TILES):
                    lower = ~masks.odd(j) if colour else masks.odd(j)
                    other.append(jnp.where(lower, behind[j], row_roll(tiles[j], -WINDOW)))
            at = colour * 5 * 18 + i
            write(moved, at, other)
            write(moved, at + 18, y_ahead(tiles, masks))
            write(moved, at + 36, y_behind(tiles, masks))
            write(moved, at + 54, z_ahead(tiles, masks))
            write(moved, at + 72, z_behind(tiles, masks))

    def matrix_at(ref, at, group, j):
        block = [ref[at + i, group, tile_of(j)] for i in range(18)]
        return block[:9], block[9:]

    def moment_of(colour, group, j):
        them = 1 - colour
        total = None
        links = (
            (staple_link, (colour * 4 + 0) * 18),
            (staple_link, (colour * 4 + 1) * 18),
            (link, (colour * 3 + 1) * 18),
            (staple_link, (colour * 4 + 2) * 18),
            (link, (colour * 3 + 2) * 18),
            (staple_link, (colour * 4 + 3) * 18),
        )
        for number, (ref, at) in enumerate(links):
            if number == 0:
                right = matrix_at(field, them * 18, group, j)
            else:
                right = matrix_at(moved, (them * 5 + number - 1) * 18, group, j)
            total = times_dagger(total, matrix_at(ref, at, group, j), right)
        gauge = matrix_at(field, colour * 18, group, j)
        return gauge, times(gauge, total)

    def groups(body, init):
        count = rows // 8
        if count == 1:
            return body(0, pl.ds(0, 8), init)
        return lax.fori_loop(
            0, count, lambda g, carry: body(g, pl.ds(pl.multiple_of(g * 8, 8), 8), carry), init
        )

    group_masks = Masks(8)
    owned = [group_masks.owned(j, start, width) for j in range(TILES)]
    zero = jnp.zeros((8, LANES), jnp.float32)

    def half_sweep(colour):
        def body(g, group, carry):
            score, squares = carry
            for j in range(TILES):
                gauge, moment = moment_of(colour, group, j)
                for one, two in PAIRS:
                    coeffs = relax_coeffs(moment, one, two)
                    gauge = turn_rows(gauge, one, two, coeffs)
                    moment = turn_rows(moment, one, two, coeffs)
                for i in range(9):
                    field[colour * 18 + i, group, tile_of(j)] = gauge[0][i]
                    field[colour * 18 + 9 + i, group, tile_of(j)] = gauge[1][i]
                if colour == 1:
                    trace = moment[0][0] + moment[0][4] + moment[0][8]
                    score = score + jnp.where(owned[j], trace, 0.0)
                    squares = squares + jnp.where(owned[j], antihermitian_squares(moment), 0.0)
            return score, squares

        return groups(body, (zero, zero))

    move(1)

    def iteration(k, carry):
        half_sweep(0)
        move(0)
        score, squares = half_sweep(1)
        move(1)
        scores[k] = score
        scores[ITERS] = squares
        return carry

    lax.fori_loop(0, ITERS, iteration, 0)

    def theta_body(g, group, squares):
        for j in range(TILES):
            _, moment = moment_of(0, group, j)
            squares = squares + jnp.where(owned[j], antihermitian_squares(moment), 0.0)
        return squares

    scores[ITERS] = groups(theta_body, scores[ITERS])

    line = lax.broadcasted_iota(jnp.int32, (8, LANES), 0)
    sums = zero
    for k in range(ITERS + 1):
        sums = jnp.where(line == k, jnp.sum(scores[k]), sums)
    sums_out[...] = sums

    tile_line = lax.broadcasted_iota(jnp.int32, (own_tiles, LANES), 0)
    tile_lane = lax.broadcasted_iota(jnp.int32, (own_tiles, LANES), 1)
    place = tile_line * LANES + tile_lane
    odd = (place // NZ + place % NZ) % 2 == 1
    low = tile_lane < HALF
    for i in range(18):
        colours = []
        for colour in range(2):
            base = (colour * PARTS + i) * stride
            for j in range(TILES):
                flat[pl.ds(base + j, rows, stride=TILES), :] = field[colour * 18 + i, :, tile_of(j)]
            early = flat[pl.ds(base + first_own, own_tiles), :]
            late = flat[pl.ds(base + first_own + 1, own_tiles), :]
            colours.append(jnp.where(low, lane_roll(early, HALF), lane_roll(late, HALF)))
        planes = (
            jnp.where(odd, colours[1], colours[0]),
            jnp.where(odd, colours[0], colours[1]),
        )
        for x in range(2):
            for t in range(own_tiles):
                size = min(LANES, width - t * LANES)
                gauge_out[i, x : x + 1, t * LANES : t * LANES + size] = planes[x][
                    t : t + 1, :size
                ]


def sweeps(own, below, above, width):
    pairs = len(own)
    own_tiles = -(-width // LANES)
    rows = pairs * WINDOW
    stride = pairs * WINDOW * TILES
    cells = lambda count: pltpu.VMEM((count, rows, BLOCK), jnp.float32)
    return pl.pallas_call(
        lambda *refs: sweep_kernel(pairs, own_tiles, width, *refs),
        out_shape=[
            jax.ShapeDtypeStruct((18, 2, width), jnp.float32),
            jax.ShapeDtypeStruct((8, LANES), jnp.float32),
        ],
        scratch_shapes=[
            pltpu.VMEM((2 * PARTS * stride, LANES), jnp.float32),
            pltpu.VMEM((36 * rows, LANES), jnp.float32),
            cells(2 * 3 * 18),
            cells(2 * 4 * 18),
            cells(2 * 18),
            cells(2 * 5 * 18),
            pltpu.VMEM((8, 8, LANES), jnp.float32),
        ],
        compiler_params=pltpu.CompilerParams(vmem_limit_bytes=56 * 1024 * 1024),
        name="sweeps",
    )(*own, *below, *above)


def rotate_kernel(here, links, ahead, out):
    def matrix(ref):
        return [ref[i] for i in range(9)], [ref[9 + i] for i in range(9)]

    re, im = times_dagger(None, times(matrix(here), matrix(links)), matrix(ahead))
    for i in range(9):
        out[i] = re[i]
        out[9 + i] = im[i]


def rotate(here, links, ahead):
    return pl.pallas_call(
        rotate_kernel, out_shape=jax.ShapeDtypeStruct(here.shape, here.dtype), name="rotate"
    )(here, links, ahead)


def from_ahead(block, axis, distance):
    count = lax.axis_size(axis)
    return lax.ppermute(block, axis, [((i + distance) % count, i) for i in range(count)])


def local(space_links, time_links, start_gauge):
    x_sites, width = start_gauge.shape[-2:]
    pairs = lax.axis_size("gx")
    volume = x_sites * pairs * width * lax.axis_size("gy")
    assert x_sites == 2 and start_gauge.shape[3] == 1
    assert width % NZ == 0 and (width // NZ) % 2 == 0 and width % LANES == HALF
    assert 2 * width + BLOCK == WINDOW * BLOCK and pairs >= 2
    assert BLOCK_ROWS >= 2 * ITERS

    own, below, above = pack(
        space_links.reshape(54, x_sites, width), start_gauge.reshape(18, x_sites, width)
    )
    below = from_ahead(below, "gy", -1)
    above = from_ahead(above, "gy", 1)
    owns = [own] + [from_ahead(own, "gx", i) for i in range(1, pairs)]
    belows = [below] + [from_ahead(below, "gx", i) for i in range(1, pairs)]
    aboves = [above] + [from_ahead(above, "gx", i) for i in range(1, pairs)]
    gauge, sums = sweeps(owns, belows, aboves, width)
    ahead = from_ahead(gauge, "ta", 1)
    count = lax.axis_size("gy")
    step = 1
    if count & (count - 1) == 0:
        while step < count:
            sums = sums + lax.ppermute(sums, "gy", [(i, i ^ step) for i in range(count)])
            step *= 2
    else:
        sums = sums + sum(from_ahead(sums, "gy", i) for i in range(1, count))
    rotated = rotate(gauge, time_links.reshape(18, x_sites, width), ahead)
    functional = sums[:ITERS, :1] / (9.0 * volume)
    theta = sums[ITERS, :1] / (3.0 * volume)
    return (gauge.reshape(start_gauge.shape), rotated.reshape(start_gauge.shape), functional, theta)


def solution(mesh):
    placed = (
        P(None, None, None, None, "ta", "gx", "gy"),
        P(None, None, None, "ta", "gx", "gy"),
        P(None, None, None, "ta", "gx", "gy"),
    )
    return jax.shard_map(
        local,
        mesh=mesh,
        in_specs=placed,
        out_specs=(
            P(None, None, None, "ta", "gx", "gy"),
            P(None, None, None, "ta", "gx", "gy"),
            P(None, "ta"),
            P("ta"),
        ),
        check_vma=False,
    )
```

profile of v0, /device:TPU:0, one launch (start us, length us, event | category | flops | bytes accessed | tf_op | source)
XLA Modules:
  0.0 50.5 jit_solution(14348712200133827218)
XLA Ops:
  0.6 2.0 %pack.1 = (f32[480,128]{1,0:T(8,128)}, f32[312,128]{1,0:T(8,128)}, f32[304,128]{1,0:T(8,128)}) custom-call(f32[54,2,576]{2,1,0:T(2,128)} %bitcast.10, f32[18,2,576]{2,1,0:T(2,128)} %bitcast.11), custom_call_target="tpu_custom_call" | custom-call | tf_op jit(solution)/shard_map/pack/pallas_call | solution.py:83
  2.7 3.1 %collective-permute-start.1 = (f32[312,128]{1,0:T(8,128)}, f32[312,128]{1,0:T(8,128)S(1)}, u32[]{:S(2)}, u32[]{:S(2)}) collective-permute-start(f32[312,128]{1,0:T(8,128)} %get-tuple-element.10), channel_id=1, source_target_pairs={{3,0},{0,1},{1,2},{2,3},{7,4},{4,5},{5,6},{6,7},{11,8},{8,9},{9,10... | collective-permute-start | bytes 479240 | tf_op jit(solution)/shard_map/ppermute | solution.py:528
  5.7 2.0 %collective-permute-start.3 = (f32[304,128]{1,0:T(8,128)}, f32[304,128]{1,0:T(8,128)S(1)}, u32[]{:S(2)}, u32[]{:S(2)}) collective-permute-start(f32[304,128]{1,0:T(8,128)} %get-tuple-element.11), channel_id=1, source_target_pairs={{1,0},{2,1},{3,2},{0,3},{5,4},{6,5},{7,6},{4,7},{9,8},{10,9},{11,1... | collective-permute-start | bytes 466952 | tf_op jit(solution)/shard_map/ppermute | solution.py:528
  7.7 1.7 %collective-permute-start = (f32[480,128]{1,0:T(8,128)}, f32[480,128]{1,0:T(8,128)S(1)}, u32[]{:S(2)}, u32[]{:S(2)}) collective-permute-start(f32[480,128]{1,0:T(8,128)} %get-tuple-element.9.refs_0_), channel_id=1, source_target_pairs={{4,0},{0,4},{5,1},{1,5},{6,2},{2,6},{7,3},{3,7},{12,8},{8,12},{13,... | collective-permute-start | bytes 737288 | tf_op jit(solution)/shard_map/ppermute | solution.py:528
  9.5 3.5 %collective-permute-done.1.refs_2_ = f32[312,128]{1,0:T(8,128)S(1)} collective-permute-done((f32[312,128]{1,0:T(8,128)}, f32[312,128]{1,0:T(8,128)S(1)}, u32[]{:S(2)}, u32[]{:S(2)}) %collective-permute-start.1) | collective-permute-done | bytes 159776 | tf_op jit(solution)/shard_map/ppermute | solution.py:528
  13.0 0.0 copy-start.1
  13.0 1.7 %collective-permute-start.2 = (f32[312,128]{1,0:T(8,128)S(1)}, f32[312,128]{1,0:T(8,128)S(1)}, u32[]{:S(2)}, u32[]{:S(2)}) collective-permute-start(f32[312,128]{1,0:T(8,128)S(1)} %collective-permute-done.1.refs_2_), channel_id=1, source_target_pairs={{4,0},{0,4},{5,1},{1,5},{6,2},{2,6},{7,3},{3,7},{12,8},{8,12},{13,... | collective-permute-start | bytes 479240 | tf_op jit(solution)/shard_map/ppermute | solution.py:528
  14.7 0.2 collective-permute-done.3.refs_4_
  14.8 0.0 copy-start.3
  14.8 1.5 %collective-permute-start.4 = (f32[304,128]{1,0:T(8,128)S(1)}, f32[304,128]{1,0:T(8,128)S(1)}, u32[]{:S(2)}, u32[]{:S(2)}) collective-permute-start(f32[304,128]{1,0:T(8,128)S(1)} %collective-permute-done.3.refs_4_), channel_id=1, source_target_pairs={{4,0},{0,4},{5,1},{1,5},{6,2},{2,6},{7,3},{3,7},{12,8},{8,12},{13,... | collective-permute-start | bytes 466952 | tf_op jit(solution)/shard_map/ppermute | solution.py:528
  16.3 0.5 collective-permute-done.refs_1_
  16.8 0.0 copy-start
  16.8 5.3 %collective-permute-done.4.refs_5_ = f32[304,128]{1,0:T(8,128)S(1)} collective-permute-done((f32[304,128]{1,0:T(8,128)S(1)}, f32[304,128]{1,0:T(8,128)S(1)}, u32[]{:S(2)}, u32[]{:S(2)}) %collective-permute-start.4) | collective-permute-done | bytes 155680 | tf_op jit(solution)/shard_map/ppermute | solution.py:528
  22.1 0.0 copy-start.4
  22.1 0.0 collective-permute-done.2.refs_3_
  22.1 0.0 copy-done.1
  22.1 0.0 copy-done.3
  22.2 0.0 copy-done
  22.2 0.6 %copy-done.4 = f32[304,128]{1,0:T(8,128)} copy-done((f32[304,128]{1,0:T(8,128)}, f32[304,128]{1,0:T(8,128)S(1)}, u32[]{:S(2)}) %copy-start.4) | copy-done | bytes 155672
  22.8 0.0 copy-start.2
  22.8 0.7 %copy-done.2 = f32[312,128]{1,0:T(8,128)} copy-done((f32[312,128]{1,0:T(8,128)}, f32[312,128]{1,0:T(8,128)S(1)}, u32[]{:S(2)}) %copy-start.2) | copy-done | bytes 159768
  23.4 12.8 %sweeps.1 = (f32[18,2,576]{2,1,0:T(2,128)}, f32[8,128]{1,0:T(8,128)}) custom-call(f32[480,128]{1,0:T(8,128)} %get-tuple-element.9.refs_0_, f32[480,128]{1,0:T(8,128)} %copy-done, f32[312,128]{1,0:T(8,128)} %copy-done.1, f32[312,128]{1,0:T(8,128)} %copy-done.2, f32[304,128]{1,0:T(8,128)} %copy-done.3, f32[304,128]{1,0:T(8,128)} %copy-done.4), custom_call_target="tpu_custom_call" | custom-call | tf_op jit(solution)/shard_map/sweeps/pallas_call | solution.py:490
  36.2 0.0 collective-permute-start.6
  36.2 3.8 %collective-permute-done.6 = f32[8,128]{1,0:T(8,128)S(1)} collective-permute-done((f32[8,128]{1,0:T(8,128)}, f32[8,128]{1,0:T(8,128)S(1)}, u32[]{:S(2)}, u32[]{:S(2)}) %collective-permute-start.6) | collective-permute-done | bytes 4128 | tf_op jit(solution)/shard_map/ppermute | solution.py:554
  40.0 0.7 %add.6 = f32[8,128]{1,0:T(8,128)S(1)} add(f32[8,128]{1,0:T(8,128)} %get-tuple-element.13, f32[8,128]{1,0:T(8,128)S(1)} %collective-permute-done.6) | non-fusion elementwise | flops 1024 | bytes 12288 | tf_op jit(solution)/shard_map/add | solution.py:554
  40.7 0.9 %collective-permute-start.7 = (f32[8,128]{1,0:T(8,128)S(1)}, f32[8,128]{1,0:T(8,128)S(1)}, u32[]{:S(2)}, u32[]{:S(2)}) collective-permute-start(f32[8,128]{1,0:T(8,128)S(1)} %add.6), channel_id=1, source_target_pairs={{0,2},{1,3},{2,0},{3,1},{4,6},{5,7},{6,4},{7,5},{8,10},{9,11},{10,... | collective-permute-start | bytes 12296 | tf_op jit(solution)/shard_map/ppermute | solution.py:554
  41.6 0.0 collective-permute-start.5
  41.6 3.6 %collective-permute-done.7 = f32[8,128]{1,0:T(8,128)S(1)} collective-permute-done((f32[8,128]{1,0:T(8,128)S(1)}, f32[8,128]{1,0:T(8,128)S(1)}, u32[]{:S(2)}, u32[]{:S(2)}) %collective-permute-start.7) | collective-permute-done | bytes 4128 | tf_op jit(solution)/shard_map/ppermute | solution.py:554
  45.2 0.5 %slice.7 = f32[1,1]{1,0:T(1,128)} slice(f32[8,128]{1,0:T(8,128)S(1)} %add.7), slice={[4:5], [0:1]} | slice | bytes 8 | tf_op jit(solution)/shard_map/slice | solution.py:560
  45.7 0.6 %copy.9 = f32[4,1]{0,1:T(1,128)} copy(f32[4,1]{1,0:T(4,128)S(1)} %slice_multiply_fusion) | data formatting | bytes 32
  47.0 0.0 collective-permute-done.5.ahead
  47.0 0.0 copy-start.5
  47.0 0.6 %copy-done.5 = f32[18,2,576]{2,1,0:T(2,128)} copy-done((f32[18,2,576]{2,1,0:T(2,128)}, f32[18,2,576]{2,1,0:T(2,128)S(1)}, u32[]{:S(2)}) %copy-start.5) | copy-done | bytes 82968
  47.6 1.7 %rotate.1 = f32[18,2,576]{2,1,0:T(2,128)} custom-call(f32[18,2,576]{2,1,0:T(2,128)} %get-tuple-element.12.here, f32[18,2,576]{2,1,0:T(2,128)} %bitcast.12, f32[18,2,576]{2,1,0:T(2,128)} %copy-done.5), custom_call_target="tpu_custom_call" | custom-call | tf_op jit(solution)/shard_map/rotate/pallas_call | solution.py:521
  (2 shorter events, 0.0 us)
Async XLA Ops:
  2.7 10.3 %collective-permute-start.1 = (f32[312,128]{1,0:T(8,128)}, f32[312,128]{1,0:T(8,128)S(1)}, u32[]{:S(2)}, u32[]{:S(2)}) collective-permute-start(f32[312,128]{1,0:T(8,128)} %get-tuple-element.10), channel_id=1, source_target_pairs={{3,0},{0,1},{1,2},{2,3},{7,4},{4,5},{5,6},{6,7},{11,8},{8,9},{9,10... | collective-permute-start | bytes 479240 | tf_op jit(solution)/shard_map/ppermute | solution.py:528
  5.7 9.1 %collective-permute-start.3 = (f32[304,128]{1,0:T(8,128)}, f32[304,128]{1,0:T(8,128)S(1)}, u32[]{:S(2)}, u32[]{:S(2)}) collective-permute-start(f32[304,128]{1,0:T(8,128)} %get-tuple-element.11), channel_id=1, source_target_pairs={{1,0},{2,1},{3,2},{0,3},{5,4},{6,5},{7,6},{4,7},{9,8},{10,9},{11,1... | collective-permute-start | bytes 466952 | tf_op jit(solution)/shard_map/ppermute | solution.py:528
  7.7 9.0 %collective-permute-start = (f32[480,128]{1,0:T(8,128)}, f32[480,128]{1,0:T(8,128)S(1)}, u32[]{:S(2)}, u32[]{:S(2)}) collective-permute-start(f32[480,128]{1,0:T(8,128)} %get-tuple-element.9.refs_0_), channel_id=1, source_target_pairs={{4,0},{0,4},{5,1},{1,5},{6,2},{2,6},{7,3},{3,7},{12,8},{8,12},{13,... | collective-permute-start | bytes 737288 | tf_op jit(solution)/shard_map/ppermute | solution.py:528
  13.0 9.2 %copy-start.1 = (f32[312,128]{1,0:T(8,128)}, f32[312,128]{1,0:T(8,128)S(1)}, u32[]{:S(2)}) copy-start(f32[312,128]{1,0:T(8,128)S(1)} %collective-permute-done.1.refs_2_) | copy-start | bytes 479236
  13.0 9.2 %collective-permute-start.2 = (f32[312,128]{1,0:T(8,128)S(1)}, f32[312,128]{1,0:T(8,128)S(1)}, u32[]{:S(2)}, u32[]{:S(2)}) collective-permute-start(f32[312,128]{1,0:T(8,128)S(1)} %collective-permute-done.1.refs_2_), channel_id=1, source_target_pairs={{4,0},{0,4},{5,1},{1,5},{6,2},{2,6},{7,3},{3,7},{12,8},{8,12},{13,... | collective-permute-start | bytes 479240 | tf_op jit(solution)/shard_map/ppermute | solution.py:528
  14.8 7.3 %copy-start.3 = (f32[304,128]{1,0:T(8,128)}, f32[304,128]{1,0:T(8,128)S(1)}, u32[]{:S(2)}) copy-start(f32[304,128]{1,0:T(8,128)S(1)} %collective-permute-done.3.refs_4_) | copy-start | bytes 466948
  14.8 7.3 %collective-permute-start.4 = (f32[304,128]{1,0:T(8,128)S(1)}, f32[304,128]{1,0:T(8,128)S(1)}, u32[]{:S(2)}, u32[]{:S(2)}) collective-permute-start(f32[304,128]{1,0:T(8,128)S(1)} %collective-permute-done.3.refs_4_), channel_id=1, source_target_pairs={{4,0},{0,4},{5,1},{1,5},{6,2},{2,6},{7,3},{3,7},{12,8},{8,12},{13,... | collective-permute-start | bytes 466952 | tf_op jit(solution)/shard_map/ppermute | solution.py:528
  16.8 5.4 %copy-start = (f32[480,128]{1,0:T(8,128)}, f32[480,128]{1,0:T(8,128)S(1)}, u32[]{:S(2)}) copy-start(f32[480,128]{1,0:T(8,128)S(1)} %collective-permute-done.refs_1_) | copy-start | bytes 737284
  22.1 0.7 %copy-start.4 = (f32[304,128]{1,0:T(8,128)}, f32[304,128]{1,0:T(8,128)S(1)}, u32[]{:S(2)}) copy-start(f32[304,128]{1,0:T(8,128)S(1)} %collective-permute-done.4.refs_5_) | copy-start | bytes 466948
  22.8 0.7 %copy-start.2 = (f32[312,128]{1,0:T(8,128)}, f32[312,128]{1,0:T(8,128)S(1)}, u32[]{:S(2)}) copy-start(f32[312,128]{1,0:T(8,128)S(1)} %collective-permute-done.2.refs_3_) | copy-start | bytes 479236
  36.2 3.8 %collective-permute-start.6 = (f32[8,128]{1,0:T(8,128)}, f32[8,128]{1,0:T(8,128)S(1)}, u32[]{:S(2)}, u32[]{:S(2)}) collective-permute-start(f32[8,128]{1,0:T(8,128)} %get-tuple-element.13), channel_id=1, source_target_pairs={{0,1},{1,0},{2,3},{3,2},{4,5},{5,4},{6,7},{7,6},{8,9},{9,8},{10,11... | collective-permute-start | bytes 12296 | tf_op jit(solution)/shard_map/ppermute | solution.py:554
  40.7 4.5 %collective-permute-start.7 = (f32[8,128]{1,0:T(8,128)S(1)}, f32[8,128]{1,0:T(8,128)S(1)}, u32[]{:S(2)}, u32[]{:S(2)}) collective-permute-start(f32[8,128]{1,0:T(8,128)S(1)} %add.6), channel_id=1, source_target_pairs={{0,2},{1,3},{2,0},{3,1},{4,6},{5,7},{6,4},{7,5},{8,10},{9,11},{10,... | collective-permute-start | bytes 12296 | tf_op jit(solution)/shard_map/ppermute | solution.py:554
  41.6 5.3 %collective-permute-start.5 = (f32[18,2,576]{2,1,0:T(2,128)}, f32[18,2,576]{2,1,0:T(2,128)S(1)}, u32[]{:S(2)}, u32[]{:S(2)}) collective-permute-start(f32[18,2,576]{2,1,0:T(2,128)} %get-tuple-element.12.here), channel_id=1, source_target_pairs={{8,0},{16,8},{24,16},{0,24},{9,1},{17,9},{25,17},{1,25},{10,2},{18... | collective-permute-start | bytes 248840 | tf_op jit(solution)/shard_map/ppermute | solution.py:528
  47.0 0.6 %copy-start.5 = (f32[18,2,576]{2,1,0:T(2,128)}, f32[18,2,576]{2,1,0:T(2,128)S(1)}, u32[]{:S(2)}) copy-start(f32[18,2,576]{2,1,0:T(2,128)S(1)} %collective-permute-done.5.ahead) | copy-start | bytes 248836
where the time goes:
time: 50.7 us; the launch traced here: 50.5 us
  waiting for transfers between devices  16.8 us (33%)
  Pallas kernels  16.5 us (33%)
  starting transfers between devices  10.9 us (21%)
  local copies, waits for them, and re-layouts  3.04 us (6%)
  between operations  2.46 us (5%)
  other arithmetic  0.7 us (1%)
    pallas_call x1, Pallas kernels, sweeps(): pl.pallas_call(lambda *refs: sweep_kernel(pairs, own_tiles, width, *refs)...  12.8 us
    ppermute x6, starting transfers between devices, from_ahead(): lax.ppermute(block, axis, [((i + distance) % count, i) for i in range(cou...  9.99 us
    ppermute x6, waiting for transfers between devices, from_ahead(): lax.ppermute(block, axis, [((i + distance) % count, i) for i in range(cou...  9.47 us
    ppermute x2, waiting for transfers between devices, local(): lax.ppermute(sums, 'gy', [(i, i ^ step) for i in range(count)])  7.38 us
    unnamed x13, local copies, waits for them, and re-layouts  2.52 us
    pallas_call x1, Pallas kernels, pack(): pl.pallas_call(lambda *refs: pack_kernel(own_tiles, *refs), out_shape=sha...  2.03 us
    pallas_call x1, Pallas kernels, rotate(): pl.pallas_call(rotate_kernel, out_shape=jax.ShapeDtypeStruct(here.shape,...  1.73 us
  transfers between devices with their start and end apart: 8, of which 6 were waited for; matrix products, arithmetic and copies ran while one was open for 2% of the time, Pallas kernels for 0%

commit v1 on v0

--- a/solution.py
+++ b/solution.py
@@ -7,6 +7,7 @@
 from jax.experimental.pallas import tpu as pltpu
 from jax.sharding import PartitionSpec as P
 
+
 NZ = 48
 ITERS = 4
 
@@ -20,55 +21,153 @@
 TILES = BLOCK_ROWS * NZ // LANES
 BLOCK = BLOCK_ROWS * NZ
 WINDOW = 4
-LINK_PARTS = 36
-PARTS = 48
-GAUGE_AT = LINK_PARTS
-ROW_Y = 12
-
-
-def part_index(part):
-    matrix, rest = divmod(part, 12)
-    reim, rest = divmod(rest, 6)
-    return matrix, reim * 9 + rest
-
-
-def pack_kernel(own_tiles, links, gauge, own, below, above):
+COORDS = 8
+PARTS = 4 * COORDS
+ROW_Y = COORDS
+GAUGE_AT = 3 * COORDS
+POLE = 1e15
+NEAR_POLE = 1e-30
+
+
+def to_plane(point):
+    first, rest = point[0], point[1:]
+    square = rest[0] * rest[0]
+    for entry in rest[1:]:
+        square = square + entry * entry
+    upper = first >= 0.0
+    top = jnp.where(upper, 1.0, 1.0 - first)
+    bottom = jnp.where(upper, 1.0 + first, jnp.maximum(square, NEAR_POLE))
+    scale = top / bottom
+    plane = [scale * entry for entry in rest]
+    at_pole = (first < 0.0) & (square < NEAR_POLE)
+    plane[0] = jnp.where(at_pole, POLE, plane[0])
+    return plane
+
+
+def from_plane(plane):
+    square = plane[0] * plane[0]
+    for entry in plane[1:]:
+        square = square + entry * entry
+    scale = 2.0 / (1.0 + square)
+    return scale, [scale - 1.0] + [scale * entry for entry in plane]
+
+
+def row_and_basis(plane):
+    scale, point = from_plane(plane)
+    row = [(point[0], point[1]), (point[2], point[3]), (point[4], point[5])]
+    u = [(scale, point[1]), row[1], row[2]]
+    tilt = plane[0]
+    inverse = 1.0 / (1.0 + tilt * tilt)
+    basis = []
+    for j in (1, 2):
+        re, im = plane[2 * j - 1], plane[2 * j]
+        zr = (re + im * tilt) * inverse
+        zi = (re * tilt - im) * inverse
+        vector = []
+        for k in range(3):
+            ur, ui = u[k]
+            br = ui * zi - ur * zr
+            bi = -(ur * zi + ui * zr)
+            vector.append((1.0 + br, bi) if k == j else (br, bi))
+        basis.append(vector)
+    return row, basis
+
+
+def encode(first, second):
+    point = [part for entry in first for part in entry]
+    plane = to_plane(point)
+    _, basis = row_and_basis(plane)
+    coeffs = []
+    for vector in basis:
+        re = im = None
+        for (sr, si), (br, bi) in zip(second, vector):
+            tr = sr * br + si * bi
+            ti = si * br - sr * bi
+            re = tr if re is None else re + tr
+            im = ti if im is None else im + ti
+        coeffs += [re, im]
+    return plane + to_plane(coeffs)
+
+
+def decode(coords):
+    first, basis = row_and_basis(coords[:5])
+    _, coeffs = from_plane(coords[5:])
+    second = []
+    for k in range(3):
+        re = im = None
+        for j in range(2):
+            cr, ci = coeffs[2 * j], coeffs[2 * j + 1]
+            br, bi = basis[j][k]
+            tr = cr * br - ci * bi
+            ti = cr * bi + ci * br
+            re = tr if re is None else re + tr
+            im = ti if im is None else im + ti
+        second.append((re, im))
+    third = []
+    for i in range(3):
+        (ar, ai), (cr, ci) = first[(i + 1) % 3], first[(i + 2) % 3]
+        (br, bi), (dr, di) = second[(i + 1) % 3], second[(i + 2) % 3]
+        re = (ar * dr - ai * di) - (cr * br - ci * bi)
+        im = (cr * bi + ci * br) - (ar * di + ai * dr)
+        third.append((re, im))
+    rows = first + second + third
+    return [entry[0] for entry in rows], [entry[1] for entry in rows]
+
+
+def pack_kernel(
+    own_tiles, links_hbm, gauge_hbm, own, below, above, links, gauge, natural, coded, arrived
+):
+    copies = [pltpu.make_async_copy(gauge_hbm, gauge, arrived.at[0])]
+    copies.append(pltpu.make_async_copy(links_hbm, links, arrived.at[1]))
+    for copy in copies:
+        copy.start()
+    for copy in copies:
+        copy.wait()
     width = gauge.shape[-1]
+    last = width - (own_tiles - 1) * LANES
     lane = lax.broadcasted_iota(jnp.int32, (2, width), 1)
     odd = (lane // NZ + lane % NZ) % 2 == 1
-    low = lax.broadcasted_iota(jnp.int32, (2, LANES), 1) < HALF
-    extra_below = 0
-    extra_above = 0
+    rows = 2 * own_tiles
+    for matrix in (3, 0, 1, 2):
+        for number in range(12):
+            entry = number if number < 6 else number + 3
+            both = gauge[entry] if matrix == 3 else links[matrix * 18 + entry]
+            swapped = jnp.concatenate([both[1:2], both[0:1]], axis=0)
+            packed = jnp.where(odd, swapped, both)
+            for t in range(own_tiles):
+                tile = packed[:, t * LANES : (t + 1) * LANES]
+                if t == own_tiles - 1:
+                    tile = jnp.concatenate([tile, jnp.zeros((2, LANES - last), jnp.float32)], axis=1)
+                natural[pl.ds((matrix * 12 + number) * rows + 2 * t, 2), :] = tile
+        values = [natural[pl.ds((matrix * 12 + i) * rows, rows), :] for i in range(12)]
+        entries = [(values[i], values[6 + i]) for i in range(6)]
+        for i, value in enumerate(encode(entries[:3], entries[3:])):
+            coded[pl.ds(8 + (matrix * COORDS + i) * rows, rows), :] = value
+    low = lax.broadcasted_iota(jnp.int32, (rows, LANES), 1) < HALF
+    first = own_tiles - 1 - TILES
+    extra_below = extra_above = PARTS * TILES * 2
     for part in range(PARTS):
-        matrix, entry = part_index(part)
-        both = links[matrix * 18 + entry] if matrix < 3 else gauge[entry]
-        swapped = jnp.concatenate([both[1:2], both[0:1]], axis=0)
-        packed = jnp.where(odd, swapped, both)
-        last = width - (own_tiles - 1) * LANES
-        tiles = [packed[:, t * LANES : (t + 1) * LANES] for t in range(own_tiles - 1)]
-        tiles.append(
-            jnp.concatenate(
-                [packed[:, width - last :], jnp.zeros((2, LANES - last), jnp.float32)], axis=1
-            )
+        base = 8 + part * rows
+        here = pltpu.roll(coded[pl.ds(base, rows), :], HALF, 1)
+        before = pltpu.roll(coded[pl.ds(base - 2, rows), :], HALF, 1)
+        own[pl.ds(part * rows, rows), :] = jnp.where(low, before, here)
+        at = part * TILES * 2
+        edge = jnp.where(
+            low[:2],
+            coded[pl.ds(base + 2 * (own_tiles - 1), 2), :],
+            coded[pl.ds(base + 2 * first, 2), :],
         )
-        turned = [pltpu.roll(tile, HALF, 1) for tile in tiles]
-        for t in range(own_tiles):
-            shifted = jnp.where(low, turned[t - 1] if t else turned[0], turned[t])
-            own[pl.ds((part * own_tiles + t) * 2, 2), :] = shifted
-        first = own_tiles - 1 - TILES
-        edge = jnp.where(low, tiles[own_tiles - 1], tiles[first])
-        for t in range(TILES):
-            body = edge if t == 0 else tiles[first + t]
-            below[pl.ds((part * TILES + t) * 2, 2), :] = body
-            above[pl.ds((part * TILES + t) * 2, 2), :] = tiles[t]
-        if ROW_Y <= part < ROW_Y + 12 or part >= GAUGE_AT:
-            below[pl.ds(PARTS * TILES * 2 + extra_below, 1), :] = tiles[first][1:2]
+        below[pl.ds(at, 2), :] = edge
+        below[pl.ds(at + 2, 2 * TILES - 2), :] = coded[
+            pl.ds(base + 2 * first + 2, 2 * TILES - 2), :
+        ]
+        above[pl.ds(at, 2 * TILES), :] = coded[pl.ds(base, 2 * TILES), :]
+        if ROW_Y <= part < ROW_Y + COORDS or part >= GAUGE_AT:
+            below[pl.ds(extra_below, 1), :] = coded[pl.ds(base + 2 * first + 1, 1), :]
             extra_below += 1
         if part >= GAUGE_AT:
-            above[pl.ds(PARTS * TILES * 2 + extra_above, 1), :] = tiles[TILES][1:2]
+            above[pl.ds(extra_above, 1), :] = coded[pl.ds(base + 2 * TILES + 1, 1), :]
             extra_above += 1
-    rest = above.shape[0] - (PARTS * TILES * 2 + extra_above)
-    above[pl.ds(above.shape[0] - rest, rest), :] = jnp.zeros((rest, LANES), jnp.float32)
 
 
 def pack(links, gauge):
@@ -77,12 +176,21 @@
     rows = PARTS * TILES * 2
     shapes = [
         jax.ShapeDtypeStruct((PARTS * own_tiles * 2, LANES), jnp.float32),
-        jax.ShapeDtypeStruct((rows + 24, LANES), jnp.float32),
-        jax.ShapeDtypeStruct((rows + 16, LANES), jnp.float32),
+        jax.ShapeDtypeStruct((rows + 2 * COORDS, LANES), jnp.float32),
+        jax.ShapeDtypeStruct((rows + COORDS, LANES), jnp.float32),
     ]
     return pl.pallas_call(
         lambda *refs: pack_kernel(own_tiles, *refs),
         out_shape=shapes,
+        in_specs=[pl.BlockSpec(memory_space=pltpu.HBM)] * 2,
+        scratch_shapes=[
+            pltpu.VMEM(links.shape, links.dtype),
+            pltpu.VMEM(gauge.shape, gauge.dtype),
+            pltpu.VMEM((48 * own_tiles * 2, LANES), jnp.float32),
+            pltpu.VMEM((8 + PARTS * own_tiles * 2, LANES), jnp.float32),
+            pltpu.SemaphoreType.DMA((2,)),
+        ],
+        compiler_params=pltpu.CompilerParams(vmem_limit_bytes=6 << 20),
         name="pack",
     )(links, gauge)
 
@@ -97,7 +205,6 @@
 
 class Masks:
     def __init__(self, rows):
-        self.rows = rows
         self.lane = lax.broadcasted_iota(jnp.int32, (rows, LANES), 1)
         self.block = lax.broadcasted_iota(jnp.int32, (rows, LANES), 0) % WINDOW
 
@@ -160,27 +267,42 @@
     return slice(j * LANES, (j + 1) * LANES)
 
 
-def times_dagger(total, left, right):
+def times_dagger(left, right):
     left_re, left_im = left
     right_re, right_im = right
     out_re = []
     out_im = []
     for a in range(3):
         for b in range(3):
-            re = None if total is None else total[0][3 * a + b]
-            im = None if total is None else total[1][3 * a + b]
+            re = im = None
             for c in range(3):
                 lr, li = left_re[3 * a + c], left_im[3 * a + c]
                 rr, ri = right_re[3 * b + c], right_im[3 * b + c]
-                term = lr * rr
-                re = term if re is None else re + term
+                re = lr * rr if re is None else re + lr * rr
                 re = re + li * ri
-                term = li * rr
-                im = term if im is None else im + term
+                im = li * rr if im is None else im + li * rr
                 im = im - lr * ri
             out_re.append(re)
             out_im.append(im)
     return out_re, out_im
+
+
+def add_staple(sums, link, gauge):
+    gauge_re, gauge_im = gauge
+    both = [gauge_re[i] + gauge_im[i] for i in range(9)]
+    right = (both, gauge_im, gauge_re)
+    out = []
+    for k in range(3):
+        entries = []
+        for a in range(3):
+            for b in range(3):
+                value = None if sums is None else sums[k][3 * a + b]
+                for c in range(3):
+                    term = link[k][3 * a + c] * right[k][3 * b + c]
+                    value = term if value is None else value + term
+                entries.append(value)
+        out.append(entries)
+    return out
 
 
 def times(left, right):
@@ -257,7 +379,7 @@
     rows = pairs * WINDOW
     per_pair = WINDOW * TILES
     stride = pairs * per_pair
-    start = WINDOW * BLOCK - width - (WINDOW * BLOCK - 2 * width)
+    start = width
     first_own = start // LANES
     masks = Masks(rows)
 
@@ -275,11 +397,11 @@
                     pl.ds(part * TILES * 2 + colour, TILES, stride=2), :
                 ]
     for p in range(pairs):
-        for i in range(24):
+        for i in range(2 * COORDS):
             extra[pl.ds(i * rows + WINDOW * p, 1), :] = below[p][pl.ds(PARTS * TILES * 2 + i, 1), :]
-        for i in range(12):
+        for i in range(COORDS):
             ahead = WINDOW * ((p + 1) % pairs)
-            extra[pl.ds((24 + i) * rows + ahead, 1), :] = above[p][
+            extra[pl.ds((2 * COORDS + i) * rows + ahead, 1), :] = above[p][
                 pl.ds(PARTS * TILES * 2 + i, 1), :
             ]
 
@@ -291,17 +413,17 @@
     def loaded(colour, part, j):
         base = (colour * PARTS + part) * stride
         value = flat[pl.ds(base + j, rows, stride=TILES), :]
-        edge_y = ROW_Y <= part < ROW_Y + 12
+        edge_y = ROW_Y <= part < ROW_Y + COORDS
         edge_g = part >= GAUGE_AT
         if j == 0:
             fill = jnp.zeros_like(value)
             if colour == 1 and edge_g:
-                fill = extra[pl.ds((24 + part - GAUGE_AT) * rows, rows), :]
+                fill = extra[pl.ds((2 * COORDS + part - GAUGE_AT) * rows, rows), :]
             value = jnp.where(first_block, fill, value)
         if j == 1:
             value = jnp.where(low_second, row_roll(value, 1), value)
             if colour == 1 and (edge_y or edge_g):
-                at = part - ROW_Y if edge_y else 12 + part - GAUGE_AT
+                at = part - ROW_Y if edge_y else COORDS + part - GAUGE_AT
                 value = jnp.where(low_first, extra[pl.ds(at * rows, rows), :], value)
         return value
 
@@ -310,19 +432,11 @@
             target = link if matrix < 3 else field
             at = (colour * 3 + matrix) * 18 if matrix < 3 else colour * 18
             for j in range(TILES):
-                parts = [loaded(colour, matrix * 12 + i, j) for i in range(12)]
-                ar, br = parts[0:3], parts[3:6]
-                ai, bi = parts[6:9], parts[9:12]
-                for i in range(3):
-                    target[at + i, :, tile_of(j)] = ar[i]
-                    target[at + 3 + i, :, tile_of(j)] = br[i]
-                    target[at + 9 + i, :, tile_of(j)] = ai[i]
-                    target[at + 12 + i, :, tile_of(j)] = bi[i]
-                    k, n = (i + 1) % 3, (i + 2) % 3
-                    third_re = (ar[k] * br[n] - ai[k] * bi[n]) - (ar[n] * br[k] - ai[n] * bi[k])
-                    third_im = (ar[n] * bi[k] + ai[n] * br[k]) - (ar[k] * bi[n] + ai[k] * br[n])
-                    target[at + 6 + i, :, tile_of(j)] = third_re
-                    target[at + 15 + i, :, tile_of(j)] = third_im
+                coords = [loaded(colour, matrix * COORDS + i, j) for i in range(COORDS)]
+                re, im = decode(coords)
+                for i in range(9):
+                    target[at + i, :, tile_of(j)] = re[i]
+                    target[at + 9 + i, :, tile_of(j)] = im[i]
 
     def read(ref, at):
         return [ref[at, :, tile_of(j)] for j in range(TILES)]
@@ -331,28 +445,37 @@
         for j in range(TILES):
             ref[at, :, tile_of(j)] = tiles[j]
 
+    def keep(colour, direction, entry, re, im):
+        at = (colour * 6 + direction) * 27 + entry
+        write(staple_link, at, re)
+        write(staple_link, at + 9, [im[j] - re[j] for j in range(TILES)])
+        write(staple_link, at + 18, [im[j] + re[j] for j in range(TILES)])
+
     for colour in range(2):
-        for reim in range(2):
-            for a in range(3):
-                for c in range(3):
-                    here = reim * 9 + 3 * a + c
-                    there = reim * 9 + 3 * c + a
-                    sign = -1.0 if reim else 1.0
-                    ours = read(link, (colour * 3) * 18 + here)
-                    theirs = [sign * t for t in read(link, ((1 - colour) * 3) * 18 + there)]
+        for a in range(3):
+            for c in range(3):
+                here = 3 * a + c
+                there = 3 * c + a
+                same = []
+                other = []
+                for reim in range(2):
+                    ours = read(link, colour * 3 * 18 + reim * 9 + here)
+                    theirs = read(link, (1 - colour) * 3 * 18 + reim * 9 + there)
+                    if reim:
+                        theirs = [-t for t in theirs]
                     behind = [row_roll(t, WINDOW) for t in theirs]
-                    same = []
-                    other = []
-                    for j in range(TILES):
-                        lower = masks.odd(j) if colour else ~masks.odd(j)
-                        same.append(jnp.where(lower, ours[j], theirs[j]))
-                        other.append(jnp.where(lower, behind[j], ours[j]))
-                    write(staple_link, (colour * 4 + 0) * 18 + here, same)
-                    write(staple_link, (colour * 4 + 1) * 18 + here, other)
-                    theirs = [sign * t for t in read(link, ((1 - colour) * 3 + 1) * 18 + there)]
-                    write(staple_link, (colour * 4 + 2) * 18 + here, y_behind(theirs, masks))
-                    theirs = [sign * t for t in read(link, ((1 - colour) * 3 + 2) * 18 + there)]
-                    write(staple_link, (colour * 4 + 3) * 18 + here, z_behind(theirs, masks))
+                    lower = [masks.odd(j) if colour else ~masks.odd(j) for j in range(TILES)]
+                    same.append([jnp.where(lower[j], ours[j], theirs[j]) for j in range(TILES)])
+                    other.append([jnp.where(lower[j], behind[j], ours[j]) for j in range(TILES)])
+                keep(colour, 0, here, *same)
+                keep(colour, 1, here, *other)
+                for axis, shift in ((1, y_behind), (2, z_behind)):
+                    at = (colour * 3 + axis) * 18 + here
+                    keep(colour, 2 * axis, here, read(link, at), read(link, at + 9))
+                    at = ((1 - colour) * 3 + axis) * 18 + there
+                    re = shift(read(link, at), masks)
+                    im = [-t for t in shift(read(link, at + 9), masks)]
+                    keep(colour, 2 * axis + 1, here, re, im)
 
     def move(colour):
         for i in range(18):
@@ -378,21 +501,19 @@
 
     def moment_of(colour, group, j):
         them = 1 - colour
-        total = None
-        links = (
-            (staple_link, (colour * 4 + 0) * 18),
-            (staple_link, (colour * 4 + 1) * 18),
-            (link, (colour * 3 + 1) * 18),
-            (staple_link, (colour * 4 + 2) * 18),
-            (link, (colour * 3 + 2) * 18),
-            (staple_link, (colour * 4 + 3) * 18),
-        )
-        for number, (ref, at) in enumerate(links):
-            if number == 0:
+        sums = None
+        for direction in range(6):
+            if direction == 0:
                 right = matrix_at(field, them * 18, group, j)
             else:
-                right = matrix_at(moved, (them * 5 + number - 1) * 18, group, j)
-            total = times_dagger(total, matrix_at(ref, at, group, j), right)
+                right = matrix_at(moved, (them * 5 + direction - 1) * 18, group, j)
+            at = (colour * 6 + direction) * 27
+            entries = [staple_link[at + i, group, tile_of(j)] for i in range(27)]
+            sums = add_staple(sums, (entries[:9], entries[9:18], entries[18:]), right)
+        total = (
+            [sums[0][i] + sums[1][i] for i in range(9)],
+            [sums[2][i] - sums[0][i] for i in range(9)],
+        )
         gauge = matrix_at(field, colour * 18, group, j)
         return gauge, times(gauge, total)
 
@@ -408,7 +529,7 @@
     owned = [group_masks.owned(j, start, width) for j in range(TILES)]
     zero = jnp.zeros((8, LANES), jnp.float32)
 
-    def half_sweep(colour):
+    def half_sweep(colour, last=False):
         def body(g, group, carry):
             score, squares = carry
             for j in range(TILES):
@@ -423,6 +544,7 @@
                 if colour == 1:
                     trace = moment[0][0] + moment[0][4] + moment[0][8]
                     score = score + jnp.where(owned[j], trace, 0.0)
+                if last:
                     squares = squares + jnp.where(owned[j], antihermitian_squares(moment), 0.0)
             return score, squares
 
@@ -433,13 +555,15 @@
     def iteration(k, carry):
         half_sweep(0)
         move(0)
-        score, squares = half_sweep(1)
+        scores[k], _ = half_sweep(1)
         move(1)
-        scores[k] = score
-        scores[ITERS] = squares
         return carry
 
-    lax.fori_loop(0, ITERS, iteration, 0)
+    lax.fori_loop(0, ITERS - 1, iteration, 0)
+    half_sweep(0)
+    move(0)
+    scores[ITERS - 1], scores[ITERS] = half_sweep(1, last=True)
+    move(1)
 
     def theta_body(g, group, squares):
         for j in range(TILES):
@@ -450,9 +574,10 @@
     scores[ITERS] = groups(theta_body, scores[ITERS])
 
     line = lax.broadcasted_iota(jnp.int32, (8, LANES), 0)
-    sums = zero
-    for k in range(ITERS + 1):
-        sums = jnp.where(line == k, jnp.sum(scores[k]), sums)
+    column = lax.broadcasted_iota(jnp.int32, (8, LANES), 1)
+    sums = jnp.where(line == 1, jnp.sum(scores[ITERS]), 0.0)
+    for k in range(ITERS):
+        sums = jnp.where((line == 0) & (column == k), jnp.sum(scores[k]), sums)
     sums_out[...] = sums
 
     tile_line = lax.broadcasted_iota(jnp.int32, (own_tiles, LANES), 0)
@@ -495,32 +620,55 @@
         ],
         scratch_shapes=[
             pltpu.VMEM((2 * PARTS * stride, LANES), jnp.float32),
-            pltpu.VMEM((36 * rows, LANES), jnp.float32),
+            pltpu.VMEM((3 * COORDS * rows, LANES), jnp.float32),
             cells(2 * 3 * 18),
-            cells(2 * 4 * 18),
+            cells(2 * 6 * 27),
             cells(2 * 18),
             cells(2 * 5 * 18),
             pltpu.VMEM((8, 8, LANES), jnp.float32),
         ],
-        compiler_params=pltpu.CompilerParams(vmem_limit_bytes=56 * 1024 * 1024),
+        compiler_params=pltpu.CompilerParams(vmem_limit_bytes=(pairs * 7 + 2) << 20),
         name="sweeps",
     )(*own, *below, *above)
 
 
-def rotate_kernel(here, links, ahead, out):
+def rotate_kernel(here, links, ahead, gauge, out):
     def matrix(ref):
         return [ref[i] for i in range(9)], [ref[9 + i] for i in range(9)]
 
-    re, im = times_dagger(None, times(matrix(here), matrix(links)), matrix(ahead))
+    gauge[...] = here[...]
+    re, im = times_dagger(times(matrix(here), matrix(links)), matrix(ahead))
     for i in range(9):
         out[i] = re[i]
         out[9 + i] = im[i]
 
 
 def rotate(here, links, ahead):
+    shape = jax.ShapeDtypeStruct(here.shape, here.dtype)
     return pl.pallas_call(
-        rotate_kernel, out_shape=jax.ShapeDtypeStruct(here.shape, here.dtype), name="rotate"
+        rotate_kernel,
+        out_shape=[shape, shape],
+        compiler_params=pltpu.CompilerParams(vmem_limit_bytes=6 << 20),
+        name="rotate",
     )(here, links, ahead)
+
+
+def finish_kernel(volume, ours, theirs, functional, theta):
+    total = ours[...] + theirs[...]
+    functional[...] = total[:1, :ITERS] * (1.0 / (9.0 * volume))
+    theta[...] = total[1:2, :1] * (1.0 / (3.0 * volume))
+
+
+def finish(ours, theirs, volume):
+    return pl.pallas_call(
+        lambda *refs: finish_kernel(volume, *refs),
+        out_shape=[
+            jax.ShapeDtypeStruct((1, ITERS), jnp.float32),
+            jax.ShapeDtypeStruct((1, 1), jnp.float32),
+        ],
+        compiler_params=pltpu.CompilerParams(vmem_limit_bytes=1 << 20),
+        name="finish",
+    )(ours, theirs)
 
 
 def from_ahead(block, axis, distance):
@@ -528,7 +676,7 @@
     return lax.ppermute(block, axis, [((i + distance) % count, i) for i in range(count)])
 
 
-def local(space_links, time_links, start_gauge):
+def fixed(space_links, time_links, start_gauge):
     x_sites, width = start_gauge.shape[-2:]
     pairs = lax.axis_size("gx")
     volume = x_sites * pairs * width * lax.axis_size("gy")
@@ -542,23 +690,28 @@
     )
     below = from_ahead(below, "gy", -1)
     above = from_ahead(above, "gy", 1)
-    owns = [own] + [from_ahead(own, "gx", i) for i in range(1, pairs)]
-    belows = [below] + [from_ahead(below, "gx", i) for i in range(1, pairs)]
-    aboves = [above] + [from_ahead(above, "gx", i) for i in range(1, pairs)]
+    owns, belows, aboves = [own], [below], [above]
+    for i in range(1, pairs):
+        owns.append(from_ahead(own, "gx", i))
+        belows.append(from_ahead(below, "gx", i))
+        aboves.append(from_ahead(above, "gx", i))
     gauge, sums = sweeps(owns, belows, aboves, width)
     ahead = from_ahead(gauge, "ta", 1)
     count = lax.axis_size("gy")
-    step = 1
+    theirs = jnp.zeros_like(sums)
     if count & (count - 1) == 0:
+        step = 1
         while step < count:
-            sums = sums + lax.ppermute(sums, "gy", [(i, i ^ step) for i in range(count)])
+            theirs = lax.ppermute(sums, "gy", [(i, i ^ step) for i in range(count)])
             step *= 2
+            if step < count:
+                sums = sums + theirs
     else:
-        sums = sums + sum(from_ahead(sums, "gy", i) for i in range(1, count))
-    rotated = rotate(gauge, time_links.reshape(18, x_sites, width), ahead)
-    functional = sums[:ITERS, :1] / (9.0 * volume)
-    theta = sums[ITERS, :1] / (3.0 * volume)
-    return (gauge.reshape(start_gauge.shape), rotated.reshape(start_gauge.shape), functional, theta)
+        theirs = sum(from_ahead(sums, "gy", i) for i in range(1, count))
+    gauge, rotated = rotate(gauge, time_links.reshape(18, x_sites, width), ahead)
+    functional, theta = finish(sums, theirs, volume)
+    shape = start_gauge.shape
+    return gauge.reshape(shape), rotated.reshape(shape), functional.reshape(ITERS, 1), theta.reshape(1)
 
 
 def solution(mesh):
@@ -568,7 +721,7 @@
         P(None, None, None, "ta", "gx", "gy"),
     )
     return jax.shard_map(
-        local,
+        fixed,
         mesh=mesh,
         in_specs=placed,
         out_specs=(

time: 50.7 us -> 37.4 us (0.74)
  Pallas kernels: 16.5 us -> 11.2 us
  waiting for transfers between devices: 16.8 us -> 12.1 us
  between operations: 2.46 us -> 0.67 us
  local copies, waits for them, and re-layouts: 3.04 us -> 1.84 us
  other arithmetic: 0.7 us -> 0.01 us
    pallas_call x1, Pallas kernels: 12.8 us -> 9.26 us  [sweeps(): pl.pallas_call(lambda *refs: sweep_kernel(pairs, own_tiles, width, *refs)...]
    ppermute x6, waiting for transfers between devices: 9.47 us -> 6.19 us  [from_ahead(): lax.ppermute(block, axis, [((i + distance) % count, i) for i in range(cou...]
    ppermute x2, waiting for transfers between devices: 7.38 us -> 5.94 us  [fixed(): theirs = lax.ppermute(sums, 'gy', [(i, i ^ step) for i in range(count)])]
    pallas_call x1, Pallas kernels: 2.03 us -> 0.62 us  [pack(): pl.pallas_call(lambda *refs: pack_kernel(own_tiles, *refs), out_shape=sha...]
    ppermute x2, starting transfers between devices: 0.94 us -> 2.24 us  [fixed(): theirs = lax.ppermute(sums, 'gy', [(i, i ^ step) for i in range(count)])]
    ppermute x6, starting transfers between devices: 9.99 us -> 9.2 us  [from_ahead(): lax.ppermute(block, axis, [((i + distance) % count, i) for i in range(cou...]
    add x2 -> x1, other arithmetic: 0.69 us -> 0.01 us  [fixed(): sums = sums + theirs]
    unnamed x13 -> x6, local copies, waits for them, and re-layouts: 2.52 us -> 1.84 us
  transfers between devices with their start and end apart: 8 -> 8, of which waited for: 6 -> 5; matrix products, arithmetic and copies ran while one was open for 2% -> 0% of each run, Pallas kernels for 0% -> 1%
where the time goes in v1:
time: 37.4 us; the launch traced here: 37.2 us
  waiting for transfers between devices  12.1 us (32%)
  starting transfers between devices  11.4 us (30%)
  Pallas kernels  11.2 us (30%)
  local copies, waits for them, and re-layouts  1.84 us (5%)
  between operations  0.67 us (2%)
    pallas_call x1, Pallas kernels, sweeps(): pl.pallas_call(lambda *refs: sweep_kernel(pairs, own_tiles, width, *refs)...  9.26 us
    ppermute x6, starting transfers between devices, from_ahead(): lax.ppermute(block, axis, [((i + distance) % count, i) for i in range(cou...  9.2 us
    ppermute x6, waiting for transfers between devices, from_ahead(): lax.ppermute(block, axis, [((i + distance) % count, i) for i in range(cou...  6.19 us
    ppermute x2, waiting for transfers between devices, fixed(): theirs = lax.ppermute(sums, 'gy', [(i, i ^ step) for i in range(count)])  5.94 us
    ppermute x2, starting transfers between devices, fixed(): theirs = lax.ppermute(sums, 'gy', [(i, i ^ step) for i in range(count)])  2.24 us
    unnamed x6, local copies, waits for them, and re-layouts  1.84 us
    pallas_call x1, Pallas kernels, rotate(): pl.pallas_call(rotate_kernel, out_shape=[shape, shape], compiler_params=p...  0.76 us
  transfers between devices with their start and end apart: 8, of which 5 were waited for; matrix products, arithmetic and copies ran while one was open for 0% of the time, Pallas kernels for 1%

profile of v1, /device:TPU:0, one launch (start us, length us, event | category | flops | bytes accessed | tf_op | source)
XLA Modules:
  0.0 37.2 jit_solution(4726903208699345523)
XLA Ops:
  0.6 0.0 copy-start
  0.6 0.9 %copy-done = f32[3,2,3,3,1,2,576]{6,5,4,3,2,1,0:T(2,128)S(1)} copy-done((f32[3,2,3,3,1,2,576]{6,5,4,3,2,1,0:T(2,128)S(1)}, f32[3,2,3,3,1,2,576]{6,5,4,3,2,1,0:T(2,128)}, u32[]{:S(2)}) %copy-start) | copy-done | bytes 248856
  1.6 0.0 copy-start.1
  1.6 0.9 %copy-done.1 = f32[2,3,3,1,2,576]{5,4,3,2,1,0:T(2,128)S(1)} copy-done((f32[2,3,3,1,2,576]{5,4,3,2,1,0:T(2,128)S(1)}, f32[2,3,3,1,2,576]{5,4,3,2,1,0:T(2,128)}, u32[]{:S(2)}) %copy-start.1) | copy-done | bytes 82968
  2.5 0.6 %pack.1 = (f32[320,128]{1,0:T(8,128)S(1)}, f32[208,128]{1,0:T(8,128)S(1)}, f32[200,128]{1,0:T(8,128)S(1)}) custom-call(f32[54,2,576]{2,1,0:T(2,128)S(1)} %bitcast.11, f32[18,2,576]{2,1,0:T(2,128)S(1)} %bitcast.12), custom_call_target="tpu_custom_call" | custom-call | tf_op jit(solution)/shard_map/pack/pallas_call | solution.py:182
  3.1 3.1 %collective-permute-start.1 = (f32[208,128]{1,0:T(8,128)S(1)}, f32[208,128]{1,0:T(8,128)S(1)}, u32[]{:S(2)}, u32[]{:S(2)}) collective-permute-start(f32[208,128]{1,0:T(8,128)S(1)} %get-tuple-element.14), channel_id=1, source_target_pairs={{3,0},{0,1},{1,2},{2,3},{7,4},{4,5},{5,6},{6,7},{11,8},{8,9},{9,10... | collective-permute-start | bytes 319496 | tf_op jit(solution)/shard_map/ppermute | solution.py:676
  6.2 2.1 %collective-permute-start.3 = (f32[200,128]{1,0:T(8,128)S(1)}, f32[200,128]{1,0:T(8,128)S(1)}, u32[]{:S(2)}, u32[]{:S(2)}) collective-permute-start(f32[200,128]{1,0:T(8,128)S(1)} %get-tuple-element.15), channel_id=1, source_target_pairs={{1,0},{2,1},{3,2},{0,3},{5,4},{6,5},{7,6},{4,7},{9,8},{10,9},{11,1... | collective-permute-start | bytes 307208 | tf_op jit(solution)/shard_map/ppermute | solution.py:676
  8.3 0.0 copy-start.2
  8.3 1.6 %collective-permute-start = (f32[320,128]{1,0:T(8,128)S(1)}, f32[320,128]{1,0:T(8,128)S(1)}, u32[]{:S(2)}, u32[]{:S(2)}) collective-permute-start(f32[320,128]{1,0:T(8,128)S(1)} %get-tuple-element.13.refs_0_), channel_id=1, source_target_pairs={{4,0},{0,4},{5,1},{1,5},{6,2},{2,6},{7,3},{3,7},{12,8},{8,12},{13,... | collective-permute-start | bytes 491528 | tf_op jit(solution)/shard_map/ppermute | solution.py:676
  10.0 2.1 %collective-permute-done.1.refs_2_ = f32[208,128]{1,0:T(8,128)S(1)} collective-permute-done((f32[208,128]{1,0:T(8,128)S(1)}, f32[208,128]{1,0:T(8,128)S(1)}, u32[]{:S(2)}, u32[]{:S(2)}) %collective-permute-start.1) | collective-permute-done | bytes 106528 | tf_op jit(solution)/shard_map/ppermute | solution.py:676
  12.0 1.5 %collective-permute-start.2 = (f32[208,128]{1,0:T(8,128)S(1)}, f32[208,128]{1,0:T(8,128)S(1)}, u32[]{:S(2)}, u32[]{:S(2)}) collective-permute-start(f32[208,128]{1,0:T(8,128)S(1)} %collective-permute-done.1.refs_2_), channel_id=1, source_target_pairs={{4,0},{0,4},{5,1},{1,5},{6,2},{2,6},{7,3},{3,7},{12,8},{8,12},{13,... | collective-permute-start | bytes 319496 | tf_op jit(solution)/shard_map/ppermute | solution.py:676
  13.5 0.0 collective-permute-done.3.refs_4_
  13.5 0.8 %collective-permute-start.4 = (f32[200,128]{1,0:T(8,128)S(1)}, f32[200,128]{1,0:T(8,128)S(1)}, u32[]{:S(2)}, u32[]{:S(2)}) collective-permute-start(f32[200,128]{1,0:T(8,128)S(1)} %collective-permute-done.3.refs_4_), channel_id=1, source_target_pairs={{4,0},{0,4},{5,1},{1,5},{6,2},{2,6},{7,3},{3,7},{12,8},{8,12},{13,... | collective-permute-start | bytes 307208 | tf_op jit(solution)/shard_map/ppermute | solution.py:676
  14.3 0.5 %collective-permute-done.refs_1_ = f32[320,128]{1,0:T(8,128)S(1)} collective-permute-done((f32[320,128]{1,0:T(8,128)S(1)}, f32[320,128]{1,0:T(8,128)S(1)}, u32[]{:S(2)}, u32[]{:S(2)}) %collective-permute-start) | collective-permute-done | bytes 163872 | tf_op jit(solution)/shard_map/ppermute | solution.py:676
  14.9 3.6 %collective-permute-done.4.refs_5_ = f32[200,128]{1,0:T(8,128)S(1)} collective-permute-done((f32[200,128]{1,0:T(8,128)S(1)}, f32[200,128]{1,0:T(8,128)S(1)}, u32[]{:S(2)}, u32[]{:S(2)}) %collective-permute-start.4) | collective-permute-done | bytes 102432 | tf_op jit(solution)/shard_map/ppermute | solution.py:676
  18.4 0.0 collective-permute-done.2.refs_3_
  18.4 9.3 %sweeps.1 = (f32[18,2,576]{2,1,0:T(2,128)S(1)}, f32[8,128]{1,0:T(8,128)S(1)}) custom-call(f32[320,128]{1,0:T(8,128)S(1)} %get-tuple-element.13.refs_0_, f32[320,128]{1,0:T(8,128)S(1)} %collective-permute-done.refs_1_, f32[208,128]{1,0:T(8,128)S(1)} %collective-permute-done.1.refs_2_, f32[208,128]{1,0:T(8,128)S(1)} %collective-permute-done.2.refs_3_, ...), custom_call_target="tpu_custom_call" | custom-call | tf_op jit(solution)/shard_map/sweeps/pallas_call | solution.py:615
  27.7 0.1 collective-permute-start.5
  27.8 0.4 %collective-permute-start.6 = (f32[8,128]{1,0:T(8,128)S(1)}, f32[8,128]{1,0:T(8,128)S(1)}, u32[]{:S(2)}, u32[]{:S(2)}) collective-permute-start(f32[8,128]{1,0:T(8,128)S(1)} %get-tuple-element.19), channel_id=1, source_target_pairs={{0,1},{1,0},{2,3},{3,2},{4,5},{5,4},{6,7},{7,6},{8,9},{9,8},{10,11... | collective-permute-start | bytes 12296 | tf_op jit(solution)/shard_map/ppermute | solution.py:705
  28.2 3.3 %collective-permute-done.6 = f32[8,128]{1,0:T(8,128)S(1)} collective-permute-done((f32[8,128]{1,0:T(8,128)S(1)}, f32[8,128]{1,0:T(8,128)S(1)}, u32[]{:S(2)}, u32[]{:S(2)}) %collective-permute-start.6) | collective-permute-done | bytes 4128 | tf_op jit(solution)/shard_map/ppermute | solution.py:705
  31.5 1.8 %collective-permute-start.7 = (f32[8,128]{1,0:T(8,128)S(1)}, f32[8,128]{1,0:T(8,128)S(1)}, u32[]{:S(2)}, u32[]{:S(2)}) collective-permute-start(f32[8,128]{1,0:T(8,128)S(1)} %add.3.refs_0_), channel_id=1, source_target_pairs={{0,2},{1,3},{2,0},{3,1},{4,6},{5,7},{6,4},{7,5},{8,10},{9,11},{10,... | collective-permute-start | bytes 12296 | tf_op jit(solution)/shard_map/ppermute | solution.py:705
  33.3 2.7 %collective-permute-done.7.refs_1_ = f32[8,128]{1,0:T(8,128)S(1)} collective-permute-done((f32[8,128]{1,0:T(8,128)S(1)}, f32[8,128]{1,0:T(8,128)S(1)}, u32[]{:S(2)}, u32[]{:S(2)}) %collective-permute-start.7) | collective-permute-done | bytes 4128 | tf_op jit(solution)/shard_map/ppermute | solution.py:705
  36.0 0.5 %finish.1 = (f32[1,4]{1,0:T(1,128)}, f32[1,1]{1,0:T(1,128)}) custom-call(f32[8,128]{1,0:T(8,128)S(1)} %add.3.refs_0_, f32[8,128]{1,0:T(8,128)S(1)} %collective-permute-done.7.refs_1_), custom_call_target="tpu_custom_call" | custom-call | tf_op jit(solution)/shard_map/finish/pallas_call | solution.py:663
  36.5 0.0 collective-permute-done.5.ahead
  36.5 0.0 copy-done.2
  36.5 0.8 %rotate.1 = (f32[18,2,576]{2,1,0:T(2,128)}, f32[18,2,576]{2,1,0:T(2,128)}) custom-call(f32[18,2,576]{2,1,0:T(2,128)S(1)} %get-tuple-element.16.here, f32[18,2,576]{2,1,0:T(2,128)S(1)} %bitcast.13, f32[18,2,576]{2,1,0:T(2,128)S(1)} %collective-permute-done.5.ahead), custom_call_target="tpu_custom_call" | custom-call | tf_op jit(solution)/shard_map/rotate/pallas_call | solution.py:648
  (1 shorter events, 0.0 us)
Async XLA Ops:
  0.6 1.0 %copy-start = (f32[3,2,3,3,1,2,576]{6,5,4,3,2,1,0:T(2,128)S(1)}, f32[3,2,3,3,1,2,576]{6,5,4,3,2,1,0:T(2,128)}, u32[]{:S(2)}) copy-start(f32[3,2,3,3,1,2,576]{6,5,4,3,2,1,0:T(2,128)} %param.3) | copy-start | bytes 746500
  1.6 0.9 %copy-start.1 = (f32[2,3,3,1,2,576]{5,4,3,2,1,0:T(2,128)S(1)}, f32[2,3,3,1,2,576]{5,4,3,2,1,0:T(2,128)}, u32[]{:S(2)}) copy-start(f32[2,3,3,1,2,576]{5,4,3,2,1,0:T(2,128)} %param.5) | copy-start | bytes 248836
  3.1 8.9 %collective-permute-start.1 = (f32[208,128]{1,0:T(8,128)S(1)}, f32[208,128]{1,0:T(8,128)S(1)}, u32[]{:S(2)}, u32[]{:S(2)}) collective-permute-start(f32[208,128]{1,0:T(8,128)S(1)} %get-tuple-element.14), channel_id=1, source_target_pairs={{3,0},{0,1},{1,2},{2,3},{7,4},{4,5},{5,6},{6,7},{11,8},{8,9},{9,10... | collective-permute-start | bytes 319496 | tf_op jit(solution)/shard_map/ppermute | solution.py:676
  6.2 7.3 %collective-permute-start.3 = (f32[200,128]{1,0:T(8,128)S(1)}, f32[200,128]{1,0:T(8,128)S(1)}, u32[]{:S(2)}, u32[]{:S(2)}) collective-permute-start(f32[200,128]{1,0:T(8,128)S(1)} %get-tuple-element.15), channel_id=1, source_target_pairs={{1,0},{2,1},{3,2},{0,3},{5,4},{6,5},{7,6},{4,7},{9,8},{10,9},{11,1... | collective-permute-start | bytes 307208 | tf_op jit(solution)/shard_map/ppermute | solution.py:676
  8.3 28.2 %copy-start.2 = (f32[2,3,3,1,2,576]{5,4,3,2,1,0:T(2,128)S(1)}, f32[2,3,3,1,2,576]{5,4,3,2,1,0:T(2,128)}, u32[]{:S(2)}) copy-start(f32[2,3,3,1,2,576]{5,4,3,2,1,0:T(2,128)} %param.4) | copy-start | bytes 248836
  8.3 6.6 %collective-permute-start = (f32[320,128]{1,0:T(8,128)S(1)}, f32[320,128]{1,0:T(8,128)S(1)}, u32[]{:S(2)}, u32[]{:S(2)}) collective-permute-start(f32[320,128]{1,0:T(8,128)S(1)} %get-tuple-element.13.refs_0_), channel_id=1, source_target_pairs={{4,0},{0,4},{5,1},{1,5},{6,2},{2,6},{7,3},{3,7},{12,8},{8,12},{13,... | collective-permute-start | bytes 491528 | tf_op jit(solution)/shard_map/ppermute | solution.py:676
  12.0 6.4 %collective-permute-start.2 = (f32[208,128]{1,0:T(8,128)S(1)}, f32[208,128]{1,0:T(8,128)S(1)}, u32[]{:S(2)}, u32[]{:S(2)}) collective-permute-start(f32[208,128]{1,0:T(8,128)S(1)} %collective-permute-done.1.refs_2_), channel_id=1, source_target_pairs={{4,0},{0,4},{5,1},{1,5},{6,2},{2,6},{7,3},{3,7},{12,8},{8,12},{13,... | collective-permute-start | bytes 319496 | tf_op jit(solution)/shard_map/ppermute | solution.py:676
  13.5 4.9 %collective-permute-start.4 = (f32[200,128]{1,0:T(8,128)S(1)}, f32[200,128]{1,0:T(8,128)S(1)}, u32[]{:S(2)}, u32[]{:S(2)}) collective-permute-start(f32[200,128]{1,0:T(8,128)S(1)} %collective-permute-done.3.refs_4_), channel_id=1, source_target_pairs={{4,0},{0,4},{5,1},{1,5},{6,2},{2,6},{7,3},{3,7},{12,8},{8,12},{13,... | collective-permute-start | bytes 307208 | tf_op jit(solution)/shard_map/ppermute | solution.py:676
  27.7 8.8 %collective-permute-start.5 = (f32[18,2,576]{2,1,0:T(2,128)S(1)}, f32[18,2,576]{2,1,0:T(2,128)S(1)}, u32[]{:S(2)}, u32[]{:S(2)}) collective-permute-start(f32[18,2,576]{2,1,0:T(2,128)S(1)} %get-tuple-element.16.here), channel_id=1, source_target_pairs={{8,0},{16,8},{24,16},{0,24},{9,1},{17,9},{25,17},{1,25},{10,2},{18... | collective-permute-start | bytes 248840 | tf_op jit(solution)/shard_map/ppermute | solution.py:676
  27.8 3.7 %collective-permute-start.6 = (f32[8,128]{1,0:T(8,128)S(1)}, f32[8,128]{1,0:T(8,128)S(1)}, u32[]{:S(2)}, u32[]{:S(2)}) collective-permute-start(f32[8,128]{1,0:T(8,128)S(1)} %get-tuple-element.19), channel_id=1, source_target_pairs={{0,1},{1,0},{2,3},{3,2},{4,5},{5,4},{6,7},{7,6},{8,9},{9,8},{10,11... | collective-permute-start | bytes 12296 | tf_op jit(solution)/shard_map/ppermute | solution.py:705
  31.5 4.5 %collective-permute-start.7 = (f32[8,128]{1,0:T(8,128)S(1)}, f32[8,128]{1,0:T(8,128)S(1)}, u32[]{:S(2)}, u32[]{:S(2)}) collective-permute-start(f32[8,128]{1,0:T(8,128)S(1)} %add.3.refs_0_), channel_id=1, source_target_pairs={{0,2},{1,3},{2,0},{3,1},{4,6},{5,7},{6,4},{7,5},{8,10},{9,11},{10,... | collective-permute-start | bytes 12296 | tf_op jit(solution)/shard_map/ppermute | solution.py:705

commit v2 on v1

--- a/solution.py
+++ b/solution.py
@@ -117,18 +117,22 @@
 def pack_kernel(
     own_tiles, links_hbm, gauge_hbm, own, below, above, links, gauge, natural, coded, arrived
 ):
-    copies = [pltpu.make_async_copy(gauge_hbm, gauge, arrived.at[0])]
-    copies.append(pltpu.make_async_copy(links_hbm, links, arrived.at[1]))
+    copies = [
+        pltpu.make_async_copy(
+            links_hbm.at[pl.ds(18 * axis, 18)], links.at[pl.ds(18 * axis, 18)], arrived.at[axis]
+        )
+        for axis in range(3)
+    ]
+    copies.append(pltpu.make_async_copy(gauge_hbm, gauge, arrived.at[3]))
     for copy in copies:
         copy.start()
-    for copy in copies:
-        copy.wait()
     width = gauge.shape[-1]
     last = width - (own_tiles - 1) * LANES
     lane = lax.broadcasted_iota(jnp.int32, (2, width), 1)
     odd = (lane // NZ + lane % NZ) % 2 == 1
     rows = 2 * own_tiles
-    for matrix in (3, 0, 1, 2):
+    for matrix in range(4):
+        copies[matrix].wait()
         for number in range(12):
             entry = number if number < 6 else number + 3
             both = gauge[entry] if matrix == 3 else links[matrix * 18 + entry]
@@ -188,11 +192,11 @@
             pltpu.VMEM(gauge.shape, gauge.dtype),
             pltpu.VMEM((48 * own_tiles * 2, LANES), jnp.float32),
             pltpu.VMEM((8 + PARTS * own_tiles * 2, LANES), jnp.float32),
-            pltpu.SemaphoreType.DMA((2,)),
+            pltpu.SemaphoreType.DMA((4,)),
         ],
         compiler_params=pltpu.CompilerParams(vmem_limit_bytes=6 << 20),
         name="pack",
-    )(links, gauge)
+    )(*[pltpu.with_memory_space_constraint(value, pltpu.HBM) for value in (links, gauge)])
 
 
 def row_roll(value, shift):
@@ -552,33 +556,11 @@
 
     move(1)
 
-    def iteration(k, carry):
+    for k in range(ITERS):
         half_sweep(0)
         move(0)
-        scores[k], _ = half_sweep(1)
+        scores[k], scores[ITERS] = half_sweep(1, last=k == ITERS - 1)
         move(1)
-        return carry
-
-    lax.fori_loop(0, ITERS - 1, iteration, 0)
-    half_sweep(0)
-    move(0)
-    scores[ITERS - 1], scores[ITERS] = half_sweep(1, last=True)
-    move(1)
-
-    def theta_body(g, group, squares):
-        for j in range(TILES):
-            _, moment = moment_of(0, group, j)
-            squares = squares + jnp.where(owned[j], antihermitian_squares(moment), 0.0)
-        return squares
-
-    scores[ITERS] = groups(theta_body, scores[ITERS])
-
-    line = lax.broadcasted_iota(jnp.int32, (8, LANES), 0)
-    column = lax.broadcasted_iota(jnp.int32, (8, LANES), 1)
-    sums = jnp.where(line == 1, jnp.sum(scores[ITERS]), 0.0)
-    for k in range(ITERS):
-        sums = jnp.where((line == 0) & (column == k), jnp.sum(scores[k]), sums)
-    sums_out[...] = sums
 
     tile_line = lax.broadcasted_iota(jnp.int32, (own_tiles, LANES), 0)
     tile_lane = lax.broadcasted_iota(jnp.int32, (own_tiles, LANES), 1)
@@ -604,6 +586,21 @@
                 gauge_out[i, x : x + 1, t * LANES : t * LANES + size] = planes[x][
                     t : t + 1, :size
                 ]
+
+    def theta_body(g, group, squares):
+        for j in range(TILES):
+            _, moment = moment_of(0, group, j)
+            squares = squares + jnp.where(owned[j], antihermitian_squares(moment), 0.0)
+        return squares
+
+    scores[ITERS] = groups(theta_body, scores[ITERS])
+
+    line = lax.broadcasted_iota(jnp.int32, (8, LANES), 0)
+    column = lax.broadcasted_iota(jnp.int32, (8, LANES), 1)
+    sums = jnp.where(line == 1, jnp.sum(scores[ITERS]), 0.0)
+    for k in range(ITERS):
+        sums = jnp.where((line == 0) & (column == k), jnp.sum(scores[k]), sums)
+    sums_out[...] = sums
 
 
 def sweeps(own, below, above, width):

time: 37.4 us -> 35.6 us (0.952)
  local copies, waits for them, and re-layouts: 1.84 us -> 0.01 us
    unnamed x6 -> x2, local copies, waits for them, and re-layouts: 1.84 us -> 0.01 us
    pallas_call x1, Pallas kernels: 0.62 us -> 1.51 us  [pack(): pl.pallas_call(lambda *refs: pack_kernel(own_tiles, *refs), out_shape=sha...]
    pallas_call x1, Pallas kernels: 9.26 us -> 8.44 us  [sweeps(): pl.pallas_call(lambda *refs: sweep_kernel(pairs, own_tiles, width, *refs)...]
where the time goes in v2:
time: 35.6 us; the launch traced here: 35.5 us
  waiting for transfers between devices  12.1 us (34%)
  starting transfers between devices  11.4 us (32%)
  Pallas kernels  11.2 us (31%)
  between operations  0.66 us (2%)
    ppermute x6, starting transfers between devices, from_ahead(): lax.ppermute(block, axis, [((i + distance) % count, i) for i in range(cou...  9.2 us
    pallas_call x1, Pallas kernels, sweeps(): pl.pallas_call(lambda *refs: sweep_kernel(pairs, own_tiles, width, *refs)...  8.44 us
    ppermute x6, waiting for transfers between devices, from_ahead(): lax.ppermute(block, axis, [((i + distance) % count, i) for i in range(cou...  6.19 us
    ppermute x2, waiting for transfers between devices, fixed(): theirs = lax.ppermute(sums, 'gy', [(i, i ^ step) for i in range(count)])  5.94 us
    ppermute x2, starting transfers between devices, fixed(): theirs = lax.ppermute(sums, 'gy', [(i, i ^ step) for i in range(count)])  2.24 us
    pallas_call x1, Pallas kernels, pack(): pl.pallas_call(lambda *refs: pack_kernel(own_tiles, *refs), out_shape=sha...  1.51 us
    pallas_call x1, Pallas kernels, rotate(): pl.pallas_call(rotate_kernel, out_shape=[shape, shape], compiler_params=p...  0.76 us
  transfers between devices with their start and end apart: 8, of which 5 were waited for; matrix products, arithmetic and copies ran while one was open for 0% of the time, Pallas kernels for 1%

profile of v2, /device:TPU:0, one launch (start us, length us, event | category | flops | bytes accessed | tf_op | source)
XLA Modules:
  0.0 35.5 jit_solution(12075514552115403973)
XLA Ops:
  0.6 1.5 %pack.1 = (f32[320,128]{1,0:T(8,128)S(1)}, f32[208,128]{1,0:T(8,128)S(1)}, f32[200,128]{1,0:T(8,128)S(1)}) custom-call(f32[54,2,576]{2,1,0:T(2,128)} %bitcast.12, f32[18,2,576]{2,1,0:T(2,128)} %bitcast.13), custom_call_target="tpu_custom_call" | custom-call | tf_op jit(solution)/shard_map/pack/pallas_call | solution.py:186
  2.1 3.1 %collective-permute-start.1 = (f32[208,128]{1,0:T(8,128)S(1)}, f32[208,128]{1,0:T(8,128)S(1)}, u32[]{:S(2)}, u32[]{:S(2)}) collective-permute-start(f32[208,128]{1,0:T(8,128)S(1)} %get-tuple-element.14), channel_id=1, source_target_pairs={{3,0},{0,1},{1,2},{2,3},{7,4},{4,5},{5,6},{6,7},{11,8},{8,9},{9,10... | collective-permute-start | bytes 319496 | tf_op jit(solution)/shard_map/ppermute | solution.py:673
  5.2 2.1 %collective-permute-start.3 = (f32[200,128]{1,0:T(8,128)S(1)}, f32[200,128]{1,0:T(8,128)S(1)}, u32[]{:S(2)}, u32[]{:S(2)}) collective-permute-start(f32[200,128]{1,0:T(8,128)S(1)} %get-tuple-element.15), channel_id=1, source_target_pairs={{1,0},{2,1},{3,2},{0,3},{5,4},{6,5},{7,6},{4,7},{9,8},{10,9},{11,1... | collective-permute-start | bytes 307208 | tf_op jit(solution)/shard_map/ppermute | solution.py:673
  7.3 0.0 copy-start
  7.3 1.6 %collective-permute-start = (f32[320,128]{1,0:T(8,128)S(1)}, f32[320,128]{1,0:T(8,128)S(1)}, u32[]{:S(2)}, u32[]{:S(2)}) collective-permute-start(f32[320,128]{1,0:T(8,128)S(1)} %get-tuple-element.13.refs_0_), channel_id=1, source_target_pairs={{4,0},{0,4},{5,1},{1,5},{6,2},{2,6},{7,3},{3,7},{12,8},{8,12},{13,... | collective-permute-start | bytes 491528 | tf_op jit(solution)/shard_map/ppermute | solution.py:673
  9.0 2.1 %collective-permute-done.1.refs_2_ = f32[208,128]{1,0:T(8,128)S(1)} collective-permute-done((f32[208,128]{1,0:T(8,128)S(1)}, f32[208,128]{1,0:T(8,128)S(1)}, u32[]{:S(2)}, u32[]{:S(2)}) %collective-permute-start.1) | collective-permute-done | bytes 106528 | tf_op jit(solution)/shard_map/ppermute | solution.py:673
  11.1 1.5 %collective-permute-start.2 = (f32[208,128]{1,0:T(8,128)S(1)}, f32[208,128]{1,0:T(8,128)S(1)}, u32[]{:S(2)}, u32[]{:S(2)}) collective-permute-start(f32[208,128]{1,0:T(8,128)S(1)} %collective-permute-done.1.refs_2_), channel_id=1, source_target_pairs={{4,0},{0,4},{5,1},{1,5},{6,2},{2,6},{7,3},{3,7},{12,8},{8,12},{13,... | collective-permute-start | bytes 319496 | tf_op jit(solution)/shard_map/ppermute | solution.py:673
  12.6 0.0 collective-permute-done.3.refs_4_
  12.6 0.8 %collective-permute-start.4 = (f32[200,128]{1,0:T(8,128)S(1)}, f32[200,128]{1,0:T(8,128)S(1)}, u32[]{:S(2)}, u32[]{:S(2)}) collective-permute-start(f32[200,128]{1,0:T(8,128)S(1)} %collective-permute-done.3.refs_4_), channel_id=1, source_target_pairs={{4,0},{0,4},{5,1},{1,5},{6,2},{2,6},{7,3},{3,7},{12,8},{8,12},{13,... | collective-permute-start | bytes 307208 | tf_op jit(solution)/shard_map/ppermute | solution.py:673
  13.4 0.5 %collective-permute-done.refs_1_ = f32[320,128]{1,0:T(8,128)S(1)} collective-permute-done((f32[320,128]{1,0:T(8,128)S(1)}, f32[320,128]{1,0:T(8,128)S(1)}, u32[]{:S(2)}, u32[]{:S(2)}) %collective-permute-start) | collective-permute-done | bytes 163872 | tf_op jit(solution)/shard_map/ppermute | solution.py:673
  13.9 3.6 %collective-permute-done.4.refs_5_ = f32[200,128]{1,0:T(8,128)S(1)} collective-permute-done((f32[200,128]{1,0:T(8,128)S(1)}, f32[200,128]{1,0:T(8,128)S(1)}, u32[]{:S(2)}, u32[]{:S(2)}) %collective-permute-start.4) | collective-permute-done | bytes 102432 | tf_op jit(solution)/shard_map/ppermute | solution.py:673
  17.5 0.0 collective-permute-done.2.refs_3_
  17.5 8.4 %sweeps.1 = (f32[18,2,576]{2,1,0:T(2,128)S(1)}, f32[8,128]{1,0:T(8,128)S(1)}) custom-call(f32[320,128]{1,0:T(8,128)S(1)} %get-tuple-element.13.refs_0_, f32[320,128]{1,0:T(8,128)S(1)} %collective-permute-done.refs_1_, f32[208,128]{1,0:T(8,128)S(1)} %collective-permute-done.1.refs_2_, f32[208,128]{1,0:T(8,128)S(1)} %collective-permute-done.2.refs_3_, ...), custom_call_target="tpu_custom_call" | custom-call | tf_op jit(solution)/shard_map/sweeps/pallas_call | solution.py:612
  25.9 0.1 collective-permute-start.5
  26.0 0.4 %collective-permute-start.6 = (f32[8,128]{1,0:T(8,128)S(1)}, f32[8,128]{1,0:T(8,128)S(1)}, u32[]{:S(2)}, u32[]{:S(2)}) collective-permute-start(f32[8,128]{1,0:T(8,128)S(1)} %get-tuple-element.19), channel_id=1, source_target_pairs={{0,1},{1,0},{2,3},{3,2},{4,5},{5,4},{6,7},{7,6},{8,9},{9,8},{10,11... | collective-permute-start | bytes 12296 | tf_op jit(solution)/shard_map/ppermute | solution.py:702
  26.4 3.3 %collective-permute-done.6 = f32[8,128]{1,0:T(8,128)S(1)} collective-permute-done((f32[8,128]{1,0:T(8,128)S(1)}, f32[8,128]{1,0:T(8,128)S(1)}, u32[]{:S(2)}, u32[]{:S(2)}) %collective-permute-start.6) | collective-permute-done | bytes 4128 | tf_op jit(solution)/shard_map/ppermute | solution.py:702
  29.7 1.8 %collective-permute-start.7 = (f32[8,128]{1,0:T(8,128)S(1)}, f32[8,128]{1,0:T(8,128)S(1)}, u32[]{:S(2)}, u32[]{:S(2)}) collective-permute-start(f32[8,128]{1,0:T(8,128)S(1)} %add.3.refs_0_), channel_id=1, source_target_pairs={{0,2},{1,3},{2,0},{3,1},{4,6},{5,7},{6,4},{7,5},{8,10},{9,11},{10,... | collective-permute-start | bytes 12296 | tf_op jit(solution)/shard_map/ppermute | solution.py:702
  31.5 2.7 %collective-permute-done.7.refs_1_ = f32[8,128]{1,0:T(8,128)S(1)} collective-permute-done((f32[8,128]{1,0:T(8,128)S(1)}, f32[8,128]{1,0:T(8,128)S(1)}, u32[]{:S(2)}, u32[]{:S(2)}) %collective-permute-start.7) | collective-permute-done | bytes 4128 | tf_op jit(solution)/shard_map/ppermute | solution.py:702
  34.2 0.5 %finish.1 = (f32[1,4]{1,0:T(1,128)}, f32[1,1]{1,0:T(1,128)}) custom-call(f32[8,128]{1,0:T(8,128)S(1)} %add.3.refs_0_, f32[8,128]{1,0:T(8,128)S(1)} %collective-permute-done.7.refs_1_), custom_call_target="tpu_custom_call" | custom-call | tf_op jit(solution)/shard_map/finish/pallas_call | solution.py:660
  34.7 0.0 collective-permute-done.5.ahead
  34.7 0.0 copy-done
  34.7 0.8 %rotate.1 = (f32[18,2,576]{2,1,0:T(2,128)}, f32[18,2,576]{2,1,0:T(2,128)}) custom-call(f32[18,2,576]{2,1,0:T(2,128)S(1)} %get-tuple-element.16.here, f32[18,2,576]{2,1,0:T(2,128)S(1)} %bitcast.11, f32[18,2,576]{2,1,0:T(2,128)S(1)} %collective-permute-done.5.ahead), custom_call_target="tpu_custom_call" | custom-call | tf_op jit(solution)/shard_map/rotate/pallas_call | solution.py:645
  (1 shorter events, 0.0 us)
Async XLA Ops:
  2.1 8.9 %collective-permute-start.1 = (f32[208,128]{1,0:T(8,128)S(1)}, f32[208,128]{1,0:T(8,128)S(1)}, u32[]{:S(2)}, u32[]{:S(2)}) collective-permute-start(f32[208,128]{1,0:T(8,128)S(1)} %get-tuple-element.14), channel_id=1, source_target_pairs={{3,0},{0,1},{1,2},{2,3},{7,4},{4,5},{5,6},{6,7},{11,8},{8,9},{9,10... | collective-permute-start | bytes 319496 | tf_op jit(solution)/shard_map/ppermute | solution.py:673
  5.2 7.3 %collective-permute-start.3 = (f32[200,128]{1,0:T(8,128)S(1)}, f32[200,128]{1,0:T(8,128)S(1)}, u32[]{:S(2)}, u32[]{:S(2)}) collective-permute-start(f32[200,128]{1,0:T(8,128)S(1)} %get-tuple-element.15), channel_id=1, source_target_pairs={{1,0},{2,1},{3,2},{0,3},{5,4},{6,5},{7,6},{4,7},{9,8},{10,9},{11,1... | collective-permute-start | bytes 307208 | tf_op jit(solution)/shard_map/ppermute | solution.py:673
  7.3 27.4 %copy-start = (f32[2,3,3,1,2,576]{5,4,3,2,1,0:T(2,128)S(1)}, f32[2,3,3,1,2,576]{5,4,3,2,1,0:T(2,128)}, u32[]{:S(2)}) copy-start(f32[2,3,3,1,2,576]{5,4,3,2,1,0:T(2,128)} %param.4) | copy-start | bytes 248836
  7.3 6.6 %collective-permute-start = (f32[320,128]{1,0:T(8,128)S(1)}, f32[320,128]{1,0:T(8,128)S(1)}, u32[]{:S(2)}, u32[]{:S(2)}) collective-permute-start(f32[320,128]{1,0:T(8,128)S(1)} %get-tuple-element.13.refs_0_), channel_id=1, source_target_pairs={{4,0},{0,4},{5,1},{1,5},{6,2},{2,6},{7,3},{3,7},{12,8},{8,12},{13,... | collective-permute-start | bytes 491528 | tf_op jit(solution)/shard_map/ppermute | solution.py:673
  11.1 6.4 %collective-permute-start.2 = (f32[208,128]{1,0:T(8,128)S(1)}, f32[208,128]{1,0:T(8,128)S(1)}, u32[]{:S(2)}, u32[]{:S(2)}) collective-permute-start(f32[208,128]{1,0:T(8,128)S(1)} %collective-permute-done.1.refs_2_), channel_id=1, source_target_pairs={{4,0},{0,4},{5,1},{1,5},{6,2},{2,6},{7,3},{3,7},{12,8},{8,12},{13,... | collective-permute-start | bytes 319496 | tf_op jit(solution)/shard_map/ppermute | solution.py:673
  12.6 4.9 %collective-permute-start.4 = (f32[200,128]{1,0:T(8,128)S(1)}, f32[200,128]{1,0:T(8,128)S(1)}, u32[]{:S(2)}, u32[]{:S(2)}) collective-permute-start(f32[200,128]{1,0:T(8,128)S(1)} %collective-permute-done.3.refs_4_), channel_id=1, source_target_pairs={{4,0},{0,4},{5,1},{1,5},{6,2},{2,6},{7,3},{3,7},{12,8},{8,12},{13,... | collective-permute-start | bytes 307208 | tf_op jit(solution)/shard_map/ppermute | solution.py:673
  25.9 8.8 %collective-permute-start.5 = (f32[18,2,576]{2,1,0:T(2,128)S(1)}, f32[18,2,576]{2,1,0:T(2,128)S(1)}, u32[]{:S(2)}, u32[]{:S(2)}) collective-permute-start(f32[18,2,576]{2,1,0:T(2,128)S(1)} %get-tuple-element.16.here), channel_id=1, source_target_pairs={{8,0},{16,8},{24,16},{0,24},{9,1},{17,9},{25,17},{1,25},{10,2},{18... | collective-permute-start | bytes 248840 | tf_op jit(solution)/shard_map/ppermute | solution.py:673
  26.0 3.7 %collective-permute-start.6 = (f32[8,128]{1,0:T(8,128)S(1)}, f32[8,128]{1,0:T(8,128)S(1)}, u32[]{:S(2)}, u32[]{:S(2)}) collective-permute-start(f32[8,128]{1,0:T(8,128)S(1)} %get-tuple-element.19), channel_id=1, source_target_pairs={{0,1},{1,0},{2,3},{3,2},{4,5},{5,4},{6,7},{7,6},{8,9},{9,8},{10,11... | collective-permute-start | bytes 12296 | tf_op jit(solution)/shard_map/ppermute | solution.py:702
  29.7 4.5 %collective-permute-start.7 = (f32[8,128]{1,0:T(8,128)S(1)}, f32[8,128]{1,0:T(8,128)S(1)}, u32[]{:S(2)}, u32[]{:S(2)}) collective-permute-start(f32[8,128]{1,0:T(8,128)S(1)} %add.3.refs_0_), channel_id=1, source_target_pairs={{0,2},{1,3},{2,0},{3,1},{4,6},{5,7},{6,4},{7,5},{8,10},{9,11},{10,... | collective-permute-start | bytes 12296 | tf_op jit(solution)/shard_map/ppermute | solution.py:702

commit v3 on v2

--- a/solution.py
+++ b/solution.py
@@ -650,13 +650,16 @@
     )(here, links, ahead)
 
 
-def finish_kernel(volume, ours, theirs, functional, theta):
-    total = ours[...] + theirs[...]
+def finish_kernel(volume, *refs):
+    functional, theta = refs[-2:]
+    total = refs[0][...]
+    for part in refs[1:-2]:
+        total = total + part[...]
     functional[...] = total[:1, :ITERS] * (1.0 / (9.0 * volume))
     theta[...] = total[1:2, :1] * (1.0 / (3.0 * volume))
 
 
-def finish(ours, theirs, volume):
+def finish(parts, volume):
     return pl.pallas_call(
         lambda *refs: finish_kernel(volume, *refs),
         out_shape=[
@@ -665,7 +668,7 @@
         ],
         compiler_params=pltpu.CompilerParams(vmem_limit_bytes=1 << 20),
         name="finish",
-    )(ours, theirs)
+    )(*parts)
 
 
 def from_ahead(block, axis, distance):
@@ -695,18 +698,14 @@
     gauge, sums = sweeps(owns, belows, aboves, width)
     ahead = from_ahead(gauge, "ta", 1)
     count = lax.axis_size("gy")
-    theirs = jnp.zeros_like(sums)
-    if count & (count - 1) == 0:
-        step = 1
-        while step < count:
-            theirs = lax.ppermute(sums, "gy", [(i, i ^ step) for i in range(count)])
-            step *= 2
-            if step < count:
-                sums = sums + theirs
-    else:
-        theirs = sum(from_ahead(sums, "gy", i) for i in range(1, count))
+    parts = [sums]
+    for i in range(1, count):
+        if count & (count - 1) == 0:
+            parts.append(lax.ppermute(sums, "gy", [(k, k ^ i) for k in range(count)]))
+        else:
+            parts.append(from_ahead(sums, "gy", i))
     gauge, rotated = rotate(gauge, time_links.reshape(18, x_sites, width), ahead)
-    functional, theta = finish(sums, theirs, volume)
+    functional, theta = finish(parts, volume)
     shape = start_gauge.shape
     return gauge.reshape(shape), rotated.reshape(shape), functional.reshape(ITERS, 1), theta.reshape(1)
 

time: 35.6 us -> 34.9 us (0.980)
  waiting for transfers between devices: 12.1 us -> 9.17 us
  starting transfers between devices: 11.4 us -> 13.7 us
    ppermute x2 -> x3, waiting for transfers between devices: 5.94 us -> 2.98 us  [fixed(): parts.append(lax.ppermute(sums, 'gy', [(k, k ^ i) for k in range(count)]))]
    ppermute x2 -> x3, starting transfers between devices: 2.24 us -> 4.45 us  [fixed(): parts.append(lax.ppermute(sums, 'gy', [(k, k ^ i) for k in range(count)]))]
  transfers between devices with their start and end apart: 8 -> 9, of which waited for: 5 -> 5; matrix products, arithmetic and copies ran while one was open for 0% -> 0% of each run, Pallas kernels for 1% -> 2%
where the time goes in v3:
time: 34.9 us; the launch traced here: 34.7 us
  starting transfers between devices  13.7 us (39%)
  Pallas kernels  11.2 us (32%)
  waiting for transfers between devices  9.17 us (26%)
  between operations  0.66 us (2%)
    ppermute x6, starting transfers between devices, from_ahead(): lax.ppermute(block, axis, [((i + distance) % count, i) for i in range(cou...  9.2 us
    pallas_call x1, Pallas kernels, sweeps(): pl.pallas_call(lambda *refs: sweep_kernel(pairs, own_tiles, width, *refs)...  8.44 us
    ppermute x6, waiting for transfers between devices, from_ahead(): lax.ppermute(block, axis, [((i + distance) % count, i) for i in range(cou...  6.19 us
    ppermute x3, starting transfers between devices, fixed(): parts.append(lax.ppermute(sums, 'gy', [(k, k ^ i) for k in range(count)]))  4.45 us
    ppermute x3, waiting for transfers between devices, fixed(): parts.append(lax.ppermute(sums, 'gy', [(k, k ^ i) for k in range(count)]))  2.98 us
    pallas_call x1, Pallas kernels, pack(): pl.pallas_call(lambda *refs: pack_kernel(own_tiles, *refs), out_shape=sha...  1.51 us
    pallas_call x1, Pallas kernels, rotate(): pl.pallas_call(rotate_kernel, out_shape=[shape, shape], compiler_params=p...  0.76 us
  transfers between devices with their start and end apart: 9, of which 5 were waited for; matrix products, arithmetic and copies ran while one was open for 0% of the time, Pallas kernels for 2%

profile of v3, /device:TPU:0, one launch (start us, length us, event | category | flops | bytes accessed | tf_op | source)
XLA Modules:
  0.0 34.7 jit_solution(16943176350921703505)
XLA Ops:
  0.6 1.5 %pack.1 = (f32[320,128]{1,0:T(8,128)S(1)}, f32[208,128]{1,0:T(8,128)S(1)}, f32[200,128]{1,0:T(8,128)S(1)}) custom-call(f32[54,2,576]{2,1,0:T(2,128)} %bitcast.12, f32[18,2,576]{2,1,0:T(2,128)} %bitcast.13), custom_call_target="tpu_custom_call" | custom-call | tf_op jit(solution)/shard_map/pack/pallas_call | solution.py:186
  2.1 3.1 %collective-permute-start.1 = (f32[208,128]{1,0:T(8,128)S(1)}, f32[208,128]{1,0:T(8,128)S(1)}, u32[]{:S(2)}, u32[]{:S(2)}) collective-permute-start(f32[208,128]{1,0:T(8,128)S(1)} %get-tuple-element.14), channel_id=1, source_target_pairs={{3,0},{0,1},{1,2},{2,3},{7,4},{4,5},{5,6},{6,7},{11,8},{8,9},{9,10... | collective-permute-start | bytes 319496 | tf_op jit(solution)/shard_map/ppermute | solution.py:676
  5.2 2.1 %collective-permute-start.3 = (f32[200,128]{1,0:T(8,128)S(1)}, f32[200,128]{1,0:T(8,128)S(1)}, u32[]{:S(2)}, u32[]{:S(2)}) collective-permute-start(f32[200,128]{1,0:T(8,128)S(1)} %get-tuple-element.15), channel_id=1, source_target_pairs={{1,0},{2,1},{3,2},{0,3},{5,4},{6,5},{7,6},{4,7},{9,8},{10,9},{11,1... | collective-permute-start | bytes 307208 | tf_op jit(solution)/shard_map/ppermute | solution.py:676
  7.3 0.0 copy-start
  7.3 1.6 %collective-permute-start = (f32[320,128]{1,0:T(8,128)S(1)}, f32[320,128]{1,0:T(8,128)S(1)}, u32[]{:S(2)}, u32[]{:S(2)}) collective-permute-start(f32[320,128]{1,0:T(8,128)S(1)} %get-tuple-element.13.refs_0_), channel_id=1, source_target_pairs={{4,0},{0,4},{5,1},{1,5},{6,2},{2,6},{7,3},{3,7},{12,8},{8,12},{13,... | collective-permute-start | bytes 491528 | tf_op jit(solution)/shard_map/ppermute | solution.py:676
  9.0 2.1 %collective-permute-done.1.refs_2_ = f32[208,128]{1,0:T(8,128)S(1)} collective-permute-done((f32[208,128]{1,0:T(8,128)S(1)}, f32[208,128]{1,0:T(8,128)S(1)}, u32[]{:S(2)}, u32[]{:S(2)}) %collective-permute-start.1) | collective-permute-done | bytes 106528 | tf_op jit(solution)/shard_map/ppermute | solution.py:676
  11.1 1.5 %collective-permute-start.2 = (f32[208,128]{1,0:T(8,128)S(1)}, f32[208,128]{1,0:T(8,128)S(1)}, u32[]{:S(2)}, u32[]{:S(2)}) collective-permute-start(f32[208,128]{1,0:T(8,128)S(1)} %collective-permute-done.1.refs_2_), channel_id=1, source_target_pairs={{4,0},{0,4},{5,1},{1,5},{6,2},{2,6},{7,3},{3,7},{12,8},{8,12},{13,... | collective-permute-start | bytes 319496 | tf_op jit(solution)/shard_map/ppermute | solution.py:676
  12.6 0.0 collective-permute-done.3.refs_4_
  12.6 0.8 %collective-permute-start.4 = (f32[200,128]{1,0:T(8,128)S(1)}, f32[200,128]{1,0:T(8,128)S(1)}, u32[]{:S(2)}, u32[]{:S(2)}) collective-permute-start(f32[200,128]{1,0:T(8,128)S(1)} %collective-permute-done.3.refs_4_), channel_id=1, source_target_pairs={{4,0},{0,4},{5,1},{1,5},{6,2},{2,6},{7,3},{3,7},{12,8},{8,12},{13,... | collective-permute-start | bytes 307208 | tf_op jit(solution)/shard_map/ppermute | solution.py:676
  13.4 0.5 %collective-permute-done.refs_1_ = f32[320,128]{1,0:T(8,128)S(1)} collective-permute-done((f32[320,128]{1,0:T(8,128)S(1)}, f32[320,128]{1,0:T(8,128)S(1)}, u32[]{:S(2)}, u32[]{:S(2)}) %collective-permute-start) | collective-permute-done | bytes 163872 | tf_op jit(solution)/shard_map/ppermute | solution.py:676
  13.9 3.6 %collective-permute-done.4.refs_5_ = f32[200,128]{1,0:T(8,128)S(1)} collective-permute-done((f32[200,128]{1,0:T(8,128)S(1)}, f32[200,128]{1,0:T(8,128)S(1)}, u32[]{:S(2)}, u32[]{:S(2)}) %collective-permute-start.4) | collective-permute-done | bytes 102432 | tf_op jit(solution)/shard_map/ppermute | solution.py:676
  17.5 0.0 collective-permute-done.2.refs_3_
  17.5 8.4 %sweeps.1 = (f32[18,2,576]{2,1,0:T(2,128)S(1)}, f32[8,128]{1,0:T(8,128)S(1)}) custom-call(f32[320,128]{1,0:T(8,128)S(1)} %get-tuple-element.13.refs_0_, f32[320,128]{1,0:T(8,128)S(1)} %collective-permute-done.refs_1_, f32[208,128]{1,0:T(8,128)S(1)} %collective-permute-done.1.refs_2_, f32[208,128]{1,0:T(8,128)S(1)} %collective-permute-done.2.refs_3_, ...), custom_call_target="tpu_custom_call" | custom-call | tf_op jit(solution)/shard_map/sweeps/pallas_call | solution.py:612
  25.9 0.1 collective-permute-start.5
  26.0 2.9 %collective-permute-start.8 = (f32[8,128]{1,0:T(8,128)S(1)}, f32[8,128]{1,0:T(8,128)S(1)}, u32[]{:S(2)}, u32[]{:S(2)}) collective-permute-start(f32[8,128]{1,0:T(8,128)S(1)} %get-tuple-element.19.refs_0_), channel_id=1, source_target_pairs={{0,3},{1,2},{2,1},{3,0},{4,7},{5,6},{6,5},{7,4},{8,11},{9,10},{10,... | collective-permute-start | bytes 12296 | tf_op jit(solution)/shard_map/ppermute | solution.py:704
  28.9 0.0 collective-permute-start.7
  28.9 1.5 %collective-permute-start.6 = (f32[8,128]{1,0:T(8,128)S(1)}, f32[8,128]{1,0:T(8,128)S(1)}, u32[]{:S(2)}, u32[]{:S(2)}) collective-permute-start(f32[8,128]{1,0:T(8,128)S(1)} %get-tuple-element.19.refs_0_), channel_id=1, source_target_pairs={{0,1},{1,0},{2,3},{3,2},{4,5},{5,4},{6,7},{7,6},{8,9},{9,8},{10,11... | collective-permute-start | bytes 12296 | tf_op jit(solution)/shard_map/ppermute | solution.py:704
  30.4 1.0 %collective-permute-done.8.refs_3_ = f32[8,128]{1,0:T(8,128)S(1)} collective-permute-done((f32[8,128]{1,0:T(8,128)S(1)}, f32[8,128]{1,0:T(8,128)S(1)}, u32[]{:S(2)}, u32[]{:S(2)}) %collective-permute-start.8) | collective-permute-done | bytes 4128 | tf_op jit(solution)/shard_map/ppermute | solution.py:704
  31.5 2.0 %collective-permute-done.7.refs_2_ = f32[8,128]{1,0:T(8,128)S(1)} collective-permute-done((f32[8,128]{1,0:T(8,128)S(1)}, f32[8,128]{1,0:T(8,128)S(1)}, u32[]{:S(2)}, u32[]{:S(2)}) %collective-permute-start.7) | collective-permute-done | bytes 4128 | tf_op jit(solution)/shard_map/ppermute | solution.py:704
  33.4 0.0 collective-permute-done.6.refs_1_
  33.4 0.5 %finish.1 = (f32[1,4]{1,0:T(1,128)}, f32[1,1]{1,0:T(1,128)}) custom-call(f32[8,128]{1,0:T(8,128)S(1)} %get-tuple-element.19.refs_0_, f32[8,128]{1,0:T(8,128)S(1)} %collective-permute-done.6.refs_1_, f32[8,128]{1,0:T(8,128)S(1)} %collective-permute-done.7.refs_2_, f32[8,128]{1,0:T(8,128)S(1)} %collective-permute-done.8.refs_3_), custom_call_target="tpu_custom_call" | custom-call | tf_op jit(solution)/shard_map/finish/pallas_call | solution.py:663
  33.9 0.0 collective-permute-done.5.ahead
  34.0 0.0 copy-done
  34.0 0.8 %rotate.1 = (f32[18,2,576]{2,1,0:T(2,128)}, f32[18,2,576]{2,1,0:T(2,128)}) custom-call(f32[18,2,576]{2,1,0:T(2,128)S(1)} %get-tuple-element.16.here, f32[18,2,576]{2,1,0:T(2,128)S(1)} %bitcast.11, f32[18,2,576]{2,1,0:T(2,128)S(1)} %collective-permute-done.5.ahead), custom_call_target="tpu_custom_call" | custom-call | tf_op jit(solution)/shard_map/rotate/pallas_call | solution.py:645
Async XLA Ops:
  2.1 8.9 %collective-permute-start.1 = (f32[208,128]{1,0:T(8,128)S(1)}, f32[208,128]{1,0:T(8,128)S(1)}, u32[]{:S(2)}, u32[]{:S(2)}) collective-permute-start(f32[208,128]{1,0:T(8,128)S(1)} %get-tuple-element.14), channel_id=1, source_target_pairs={{3,0},{0,1},{1,2},{2,3},{7,4},{4,5},{5,6},{6,7},{11,8},{8,9},{9,10... | collective-permute-start | bytes 319496 | tf_op jit(solution)/shard_map/ppermute | solution.py:676
  5.2 7.3 %collective-permute-start.3 = (f32[200,128]{1,0:T(8,128)S(1)}, f32[200,128]{1,0:T(8,128)S(1)}, u32[]{:S(2)}, u32[]{:S(2)}) collective-permute-start(f32[200,128]{1,0:T(8,128)S(1)} %get-tuple-element.15), channel_id=1, source_target_pairs={{1,0},{2,1},{3,2},{0,3},{5,4},{6,5},{7,6},{4,7},{9,8},{10,9},{11,1... | collective-permute-start | bytes 307208 | tf_op jit(solution)/shard_map/ppermute | solution.py:676
  7.3 26.6 %copy-start = (f32[2,3,3,1,2,576]{5,4,3,2,1,0:T(2,128)S(1)}, f32[2,3,3,1,2,576]{5,4,3,2,1,0:T(2,128)}, u32[]{:S(2)}) copy-start(f32[2,3,3,1,2,576]{5,4,3,2,1,0:T(2,128)} %param.4) | copy-start | bytes 248836
  7.3 6.6 %collective-permute-start = (f32[320,128]{1,0:T(8,128)S(1)}, f32[320,128]{1,0:T(8,128)S(1)}, u32[]{:S(2)}, u32[]{:S(2)}) collective-permute-start(f32[320,128]{1,0:T(8,128)S(1)} %get-tuple-element.13.refs_0_), channel_id=1, source_target_pairs={{4,0},{0,4},{5,1},{1,5},{6,2},{2,6},{7,3},{3,7},{12,8},{8,12},{13,... | collective-permute-start | bytes 491528 | tf_op jit(solution)/shard_map/ppermute | solution.py:676
  11.1 6.4 %collective-permute-start.2 = (f32[208,128]{1,0:T(8,128)S(1)}, f32[208,128]{1,0:T(8,128)S(1)}, u32[]{:S(2)}, u32[]{:S(2)}) collective-permute-start(f32[208,128]{1,0:T(8,128)S(1)} %collective-permute-done.1.refs_2_), channel_id=1, source_target_pairs={{4,0},{0,4},{5,1},{1,5},{6,2},{2,6},{7,3},{3,7},{12,8},{8,12},{13,... | collective-permute-start | bytes 319496 | tf_op jit(solution)/shard_map/ppermute | solution.py:676
  12.6 4.9 %collective-permute-start.4 = (f32[200,128]{1,0:T(8,128)S(1)}, f32[200,128]{1,0:T(8,128)S(1)}, u32[]{:S(2)}, u32[]{:S(2)}) collective-permute-start(f32[200,128]{1,0:T(8,128)S(1)} %collective-permute-done.3.refs_4_), channel_id=1, source_target_pairs={{4,0},{0,4},{5,1},{1,5},{6,2},{2,6},{7,3},{3,7},{12,8},{8,12},{13,... | collective-permute-start | bytes 307208 | tf_op jit(solution)/shard_map/ppermute | solution.py:676
  25.9 8.0 %collective-permute-start.5 = (f32[18,2,576]{2,1,0:T(2,128)S(1)}, f32[18,2,576]{2,1,0:T(2,128)S(1)}, u32[]{:S(2)}, u32[]{:S(2)}) collective-permute-start(f32[18,2,576]{2,1,0:T(2,128)S(1)} %get-tuple-element.16.here), channel_id=1, source_target_pairs={{8,0},{16,8},{24,16},{0,24},{9,1},{17,9},{25,17},{1,25},{10,2},{18... | collective-permute-start | bytes 248840 | tf_op jit(solution)/shard_map/ppermute | solution.py:676
  26.0 5.5 %collective-permute-start.8 = (f32[8,128]{1,0:T(8,128)S(1)}, f32[8,128]{1,0:T(8,128)S(1)}, u32[]{:S(2)}, u32[]{:S(2)}) collective-permute-start(f32[8,128]{1,0:T(8,128)S(1)} %get-tuple-element.19.refs_0_), channel_id=1, source_target_pairs={{0,3},{1,2},{2,1},{3,0},{4,7},{5,6},{6,5},{7,4},{8,11},{9,10},{10,... | collective-permute-start | bytes 12296 | tf_op jit(solution)/shard_map/ppermute | solution.py:704
  28.9 4.5 %collective-permute-start.7 = (f32[8,128]{1,0:T(8,128)S(1)}, f32[8,128]{1,0:T(8,128)S(1)}, u32[]{:S(2)}, u32[]{:S(2)}) collective-permute-start(f32[8,128]{1,0:T(8,128)S(1)} %get-tuple-element.19.refs_0_), channel_id=1, source_target_pairs={{0,2},{1,3},{2,0},{3,1},{4,6},{5,7},{6,4},{7,5},{8,10},{9,11},{10,... | collective-permute-start | bytes 12296 | tf_op jit(solution)/shard_map/ppermute | solution.py:704
  28.9 4.5 %collective-permute-start.6 = (f32[8,128]{1,0:T(8,128)S(1)}, f32[8,128]{1,0:T(8,128)S(1)}, u32[]{:S(2)}, u32[]{:S(2)}) collective-permute-start(f32[8,128]{1,0:T(8,128)S(1)} %get-tuple-element.19.refs_0_), channel_id=1, source_target_pairs={{0,1},{1,0},{2,3},{3,2},{4,5},{5,4},{6,7},{7,6},{8,9},{9,8},{10,11... | collective-permute-start | bytes 12296 | tf_op jit(solution)/shard_map/ppermute | solution.py:704
